TPU v7x, 8 devices: a whole 2x2x1 slice. The times are simulated.
8 devices in a mesh: rep: 1 (over z), r: 2 (over y), s: 4 (over x, core).
Axes of the slice: x: 2, y: 2, z: 1, core: 2. Of those that a mesh axis runs over, the one named last changes fastest.
Arguments:
- x: bfloat16 [8, 4096, 1280], P(('rep', 'r', 's'))
- dy: bfloat16 [8, 4096, 1280], P(('rep', 'r', 's'))
- w_gate: bfloat16 [2, 1280, 3072], P(None, 's')
- w_up: bfloat16 [2, 1280, 3072], P(None, 's')
- w_down: bfloat16 [2, 3072, 1280], P(None, 's')
Outputs:
- output 1: bfloat16 [8, 4096, 1280], P(('rep', 'r', 's'))
- output 2: bfloat16 [2, 1280, 3072], P('rep', 's')
- output 3: bfloat16 [2, 1280, 3072], P('rep', 's')
- output 4: bfloat16 [2, 3072, 1280], P('rep', 's')
All inputs are finite; a program needn't handle non-finite values.
Results may differ from a plain program's by a relative error of at most 0.018.
Values are sent between devices in bfloat16 or wider.
A program may use at most 2 GiB of HBM per device.

v0:
```python
import jax
import jax.numpy as jnp
from jax import lax
from jax.sharding import PartitionSpec as P

NAMES = ("w_gate", "w_up", "w_down")


def matmul(a, w):
    return jnp.dot(a, w, preferred_element_type=jnp.float32).astype(jnp.bfloat16)


def normed(h):
    wide = h.astype(jnp.float32)
    scale = lax.rsqrt(jnp.mean(wide**2, -1, keepdims=True) + 1e-6)
    return (wide * scale).astype(jnp.bfloat16)


def layer(h, w):
    a = normed(h)
    gate = jnp.dot(a, w["w_gate"], preferred_element_type=jnp.float32)
    up = jnp.dot(a, w["w_up"], preferred_element_type=jnp.float32)
    return h + matmul((jax.nn.silu(gate) * up).astype(jnp.bfloat16), w["w_down"])


def solution(mesh):
    def fetched(weights, number):
        return {name: lax.all_gather(w[number], "s", axis=0, tiled=True) for name, w in zip(NAMES, weights, strict=True)}

    def summed(term):
        return lax.psum(lax.psum_scatter(term, "s", scatter_dimension=0, tiled=True), "r")

    def step(x, dy, *weights):
        layers = weights[0].shape[0]
        h, inputs = x[0], []
        for number in range(layers):
            inputs.append(h)
            h = layer(h, fetched(weights, number))
        by_h, mine = dy[0], [None] * layers
        for number in reversed(range(layers)):
            _, back = jax.vjp(lambda w, h: layer(h, w), fetched(weights, number), inputs[number])
            by_w, by_h = back(by_h)
            mine[number] = [summed(by_w[name]) for name in NAMES]
        return (by_h[None], *(jnp.stack([mine[number][i] for number in range(layers)]) for i in range(3)))

    states, cut = P(("rep", "r", "s"), None, None), P(None, "s", None)
    return jax.shard_map(
        step,
        mesh=mesh,
        in_specs=(states, states) + (cut,) * 3,
        out_specs=(states,) + (P("rep", "s", None),) * 3,
        check_vma=False,
    )
```

profile of v0, /device:TPU:0, one launch (start us, length us, event | category | flops | bytes accessed | tf_op | source)
XLA Modules:
  0.0 1250.8 jit_solution(16672550037078864707)
XLA Ops:
  67.2 42.2 %fusion.47 = f32[4096,3072]{1,0:T(8,128)} fusion(bf16[1,1280,3072]{2,1,0:T(8,128)(2,1)} %all-gather.13.cloned.1.call-done, bf16[1,4096,1280]{1,2,0:T(8,128)(2,1)} %copy.10, f32[4096]{0:T(1024)S(1)} %fusion.57), kind=kOutput, calls=%fused_computation.75 | convolution fusion | flops 32227983360 | bytes 68698112 | tf_op jit(solution)/shard_map/dot_general | solution.py:21
  121.5 56.6 %multiply_convert_fusion.1 = (bf16[4096,3072]{1,0:T(8,128)(2,1)}, f32[4096,3072]{1,0:T(8,128)}) fusion(f32[4096,3072]{1,0:T(8,128)} %fusion.47, bf16[1,1280,3072]{2,1,0:T(8,128)(2,1)} %all-gather.15.cloned.1.call-done, bf16[1,4096,1280]{1,2,0:T(8,128)(2,1)} %copy.10, f32[4096]{0:T(1024)S(1)} %fusion.57), kind=kOutput, calls=%fused_computation.13 | convolution fusion | flops 32303480832 | bytes 144195584 | tf_op jit(solution)/shard_map/dot_general | solution.py:22
  178.1 41.5 %fusion.18 = (f32[4096]{0:T(1024)S(1)}, bf16[4096,1280]{0,1:T(8,128)(2,1)}) fusion(bf16[4096,3072]{1,0:T(8,128)(2,1)} %get-tuple-element.20, bf16[1,3072,1280]{2,1,0:T(8,128)(2,1)} %all-gather.17.cloned.1.call-done, bf16[1,4096,1280]{1,2,0:T(8,128)(2,1)} %copy.10), kind=kOutput, calls=%fused_computation.40 | convolution fusion | flops 32238465024 | bytes 54018048 | tf_op jit(solution)/shard_map/dot_general | solution.py:10
  229.9 40.0 %convolution_convert_fusion.1 = bf16[4096,3072]{1,0:T(8,128)(2,1)} fusion(bf16[1,4096,1280]{2,1,0:T(8,128)(2,1)} %param.6, bf16[1,3072,1280]{2,1,0:T(8,128)(2,1)} %all-gather.21.cloned.1.call-done), kind=kOutput, calls=%fused_computation.32 | convolution fusion | flops 32224837632 | bytes 43515904 | tf_op jit(solution)/shard_map/transpose(jvp())/dot_general | solution.py:10
  269.9 14.7 %all-gather.23.cloned.1.call-done = bf16[1,1280,3072]{2,1,0:T(8,128)(2,1)} async-done(((bf16[1,320,3072]{2,1,0:T(8,128)(2,1)}), bf16[1,1280,3072]{2,1,0:T(8,128)(2,1)}) %all-gather.23.cloned.1.call-update) | async-done | bytes 7864336 | tf_op jit(solution)/shard_map/all_gather | solution.py:28
  284.5 42.2 %fusion.34 = f32[4096,3072]{1,0:T(8,128)} fusion(bf16[1,1280,3072]{2,1,0:T(8,128)(2,1)} %all-gather.23.cloned.1.call-done, bf16[4096,1280]{0,1:T(8,128)(2,1)} %get-tuple-element.23, f32[4096]{0:T(1024)S(1)} %fusion.58), kind=kOutput, calls=%fused_computation.62 | convolution fusion | flops 32227983360 | bytes 68698112 | tf_op jit(solution)/shard_map/jvp()/dot_general | solution.py:22
  339.2 66.8 %fusion.1 = (bf16[4096,3072]{1,0:T(8,128)(2,1)}, f32[4096,3072]{1,0:T(8,128)}) fusion(f32[4096,3072]{1,0:T(8,128)} %fusion.34, bf16[4096,3072]{1,0:T(8,128)(2,1)} %convolution_convert_fusion.1, bf16[1,1280,3072]{2,1,0:T(8,128)(2,1)} %all-gather.19.cloned.1.call-done, bf16[4096,1280]{0,1:T(8,128)(2,1)} %get-tuple-element.23, f32[4096]{0:T(1024)S(1)} %fusion.58), kind=kOutput, calls=%fused_computation.7 | convolution fusion | flops 32378978304 | bytes 169361408 | tf_op jit(solution)/shard_map/jvp()/dot_general | solution.py:21
  406.0 40.3 %convolution_convert_fusion.3 = bf16[4096,1280]{0,1:T(8,128)(2,1)} fusion(bf16[4096,3072]{1,0:T(8,128)(2,1)} %get-tuple-element.24, bf16[1,1280,3072]{2,1,0:T(8,128)(2,1)} %all-gather.19.cloned.1.call-done), kind=kOutput, calls=%fused_computation.46 | convolution fusion | flops 32212254720 | bytes 43515904 | tf_op jit(solution)/shard_map/transpose(jvp())/dot_general | solution.py:21
  446.3 48.5 %fusion.20 = (f32[4096]{0:T(1024)S(1)}, bf16[4096,1280]{0,1:T(8,128)(2,1)}) fusion(bf16[4096,1280]{0,1:T(8,128)(2,1)} %get-tuple-element.23, bf16[4096,1280]{0,1:T(8,128)(2,1)} %convolution_convert_fusion.3, bf16[1,1280,3072]{2,1,0:T(8,128)(2,1)} %all-gather.23.cloned.1.call-done, bf16[4096,3072]{1,0:T(8,128)(2,1)} %convolution_convert_fusion.1, ...), kind=kOutput, calls=%fused_computation.42 | convolution fusion | flops 32319205376 | bytes 114835456 | tf_op jit(solution)/shard_map/transpose(jvp())/dot_general | solution.py:22
  494.9 14.9 %fusion.31 = bf16[4096,1280]{0,1:T(8,128)(2,1)} fusion(bf16[4096,1280]{0,1:T(8,128)(2,1)} %get-tuple-element.23, bf16[4096,1280]{0,1:T(8,128)(2,1)} %get-tuple-element.27, bf16[1,4096,1280]{1,2,0:T(8,128)(2,1)S(1)} %copy-done, f32[4096]{0:T(1024)S(1)} %multiply_multiply_fusion.1, f32[4096]{0:T(1024)S(1)} %copy-done.8), kind=kLoop, calls=%fused_computation.59 | loop fusion | flops 36700160 | bytes 41975808 | tf_op jit(solution)/shard_map/transpose(jvp())/add_any | solution.py:14
  509.7 40.2 %convolution_convert_fusion.5 = bf16[3072,1280]{1,0:T(8,128)(2,1)} fusion(bf16[4096,3072]{1,0:T(8,128)(2,1)} %get-tuple-element.20, bf16[4096,1280]{0,1:T(8,128)(2,1)} %fusion.31), kind=kOutput, calls=%fused_computation.53 | convolution fusion | flops 32216186880 | bytes 43515904 | tf_op jit(solution)/shard_map/transpose(jvp())/dot_general | solution.py:10
  550.0 47.0 %fusion.28 = bf16[3072,1280]{1,0:T(8,128)(2,1)} fusion(f32[4096,3072]{1,0:T(8,128)} %fusion.34, bf16[1,4096,1280]{2,1,0:T(8,128)(2,1)} %param.6, f32[4096,3072]{1,0:T(8,128)} %get-tuple-element.25), kind=kOutput, calls=%fused_computation.54 | convolution fusion | flops 32291684352 | bytes 119013376 | tf_op jit(solution)/shard_map/transpose(jvp())/dot_general | solution.py:10
  597.1 72.8 %fusion.3 = (bf16[4096,3072]{1,0:T(8,128)(2,1)}, bf16[4096,3072]{1,0:T(8,128)(2,1)}) fusion(f32[4096,3072]{1,0:T(8,128)} %fusion.47, f32[4096,3072]{1,0:T(8,128)} %get-tuple-element.21, bf16[4096,1280]{0,1:T(8,128)(2,1)} %fusion.31, bf16[1,3072,1280]{2,1,0:T(8,128)(2,1)} %all-gather.17.cloned.1.call-done), kind=kOutput, calls=%fused_computation.9 | convolution fusion | flops 32375832576 | bytes 169345024 | tf_op jit(solution)/shard_map/transpose(jvp())/dot_general | solution.py:10
  669.9 43.5 %fusion.26 = bf16[1280,3072]{1,0:T(8,128)(2,1)} fusion(bf16[4096,3072]{1,0:T(8,128)(2,1)} %get-tuple-element.29, bf16[1,4096,1280]{1,2,0:T(8,128)(2,1)} %copy.10, f32[4096]{0:T(1024)S(1)} %copy-done.4, f32[4096,3072]{1,0:T(8,128)} %fusion.47), kind=kOutput, calls=%fused_computation.51 | convolution fusion | flops 32307412992 | bytes 93863936 | tf_op jit(solution)/shard_map/transpose(jvp())/dot_general | solution.py:22
  713.5 43.3 %fusion.27 = bf16[1280,3072]{1,0:T(8,128)(2,1)} fusion(bf16[4096,3072]{1,0:T(8,128)(2,1)} %convolution_convert_fusion.1, bf16[4096,1280]{0,1:T(8,128)(2,1)} %get-tuple-element.23, f32[4096]{0:T(1024)S(1)} %copy-done.9, f32[4096,3072]{1,0:T(8,128)} %get-tuple-element.25), kind=kOutput, calls=%fused_computation.52 | convolution fusion | flops 32307412992 | bytes 93863936 | tf_op jit(solution)/shard_map/transpose(jvp())/dot_general | solution.py:22
  756.9 40.2 %convolution_convert_fusion.6 = bf16[1280,3072]{1,0:T(8,128)(2,1)} fusion(bf16[4096,3072]{1,0:T(8,128)(2,1)} %get-tuple-element.24, bf16[4096,1280]{0,1:T(8,128)(2,1)} %get-tuple-element.23, f32[4096]{0:T(1024)S(1)} %copy-done.9), kind=kOutput, calls=%fused_computation.55 | convolution fusion | flops 32227983360 | bytes 43532288 | tf_op jit(solution)/shard_map/transpose(jvp())/dot_general | solution.py:21
  797.2 40.1 %convolution_convert_fusion.7 = bf16[1280,3072]{1,0:T(8,128)(2,1)} fusion(bf16[4096,3072]{1,0:T(8,128)(2,1)} %get-tuple-element.28, bf16[1,4096,1280]{1,2,0:T(8,128)(2,1)} %copy.10, f32[4096]{0:T(1024)S(1)} %copy-done.5), kind=kOutput, calls=%fused_computation.56 | convolution fusion | flops 32227983360 | bytes 43532288 | tf_op jit(solution)/shard_map/transpose(jvp())/dot_general | solution.py:21
  837.4 40.3 %convolution_convert_fusion.2 = bf16[4096,1280]{0,1:T(8,128)(2,1)} fusion(bf16[4096,3072]{1,0:T(8,128)(2,1)} %get-tuple-element.28, bf16[1,1280,3072]{2,1,0:T(8,128)(2,1)} %all-gather.13.cloned.1.call-done), kind=kOutput, calls=%fused_computation.45 | convolution fusion | flops 32212254720 | bytes 43515904 | tf_op jit(solution)/shard_map/transpose(jvp())/dot_general | solution.py:21
  877.7 24.0 %reduce-scatter.9.cloned.1.call-done = bf16[320,3072]{1,0:T(8,128)(2,1)} async-done(((bf16[1280,3072]{1,0:T(8,128)(2,1)}), bf16[320,3072]{1,0:T(8,128)(2,1)}) %reduce-scatter.9.cloned.1.call-update) | async-done | bytes 1966096 | tf_op jit(solution)/shard_map/reduce_scatter | solution.py:31
  901.7 63.4 %reduce-scatter.7.cloned.1.call-done = bf16[320,3072]{1,0:T(8,128)(2,1)} async-done(((bf16[1280,3072]{1,0:T(8,128)(2,1)}), bf16[320,3072]{1,0:T(8,128)(2,1)}) %reduce-scatter.7.cloned.1.call-update) | async-done | bytes 1966096 | tf_op jit(solution)/shard_map/reduce_scatter | solution.py:31
  965.2 48.4 %fusion.17 = (f32[4096]{0:T(1024)S(1)}, bf16[4096,1280]{0,1:T(8,128)(2,1)}) fusion(bf16[1,4096,1280]{1,2,0:T(8,128)(2,1)} %copy.10, bf16[4096,1280]{0,1:T(8,128)(2,1)} %convolution_convert_fusion.2, bf16[1,1280,3072]{2,1,0:T(8,128)(2,1)} %all-gather.15.cloned.1.call-done, bf16[4096,3072]{1,0:T(8,128)(2,1)} %get-tuple-element.29, f32[4096,3072]{1,0:T(8,128)} %fusion.47), kind=kOutput, calls=%fused_computation.39 | convolution fusion | flops 32319205376 | bytes 114835456 | tf_op jit(solution)/shard_map/transpose(jvp())/dot_general | solution.py:22
  1013.7 14.4 %fusion.30 = bf16[1,4096,1280]{1,2,0:T(8,128)(2,1)} fusion(bf16[4096,1280]{0,1:T(8,128)(2,1)} %fusion.31, bf16[4096,1280]{0,1:T(8,128)(2,1)} %get-tuple-element.31, bf16[1,4096,1280]{1,2,0:T(8,128)(2,1)S(1)} %bitcast.85, f32[4096]{0:T(1024)S(1)} %multiply_multiply_fusion, f32[4096]{0:T(1024)S(1)} %copy-done.6), kind=kLoop, calls=%fused_computation.58 | loop fusion | flops 36700160 | bytes 41975808 | tf_op jit(solution)/shard_map/broadcast_in_dim | solution.py:44
  1028.1 15.0 %copy.11 = bf16[1,4096,1280]{2,1,0:T(8,128)(2,1)} copy(bf16[1,4096,1280]{1,2,0:T(8,128)(2,1)} %fusion.30) | data formatting | bytes 20971520
  1043.1 190.6 %all-reduce.3.cloned.1.call-done = (bf16[1,320,3072]{2,1,0:T(8,128)(2,1)}, bf16[1,320,3072]{2,1,0:T(8,128)(2,1)}, bf16[1,320,3072]{2,1,0:T(8,128)(2,1)}, bf16[1,...) async-done(((bf16[1,320,3072]{2,1,0:T(8,128)(2,1)}, bf16[1,320,3072]{2,1,0:T(8,128)(2,1)}, bf16[1,320,3072]{2,1,0:T(8,128)(2,1)}, ...) | async-done | bytes 11796496 | tf_op jit(solution)/shard_map/psum | solution.py:31
  (78 shorter events, 105.4 us)
Async XLA Ops:
  7.2 60.1 %all-gather.13.cloned.1.call-start = ((), (), s32[]{:S(2)}) async-start(), calls=%async_computation.12 | async-start | bytes 9830400 | tf_op jit(solution)/shard_map/all_gather | solution.py:28
  11.6 109.9 %all-gather.15.cloned.1.call-start = ((), (), s32[]{:S(2)}) async-start(), calls=%async_computation.13 | async-start | bytes 9830400 | tf_op jit(solution)/shard_map/all_gather | solution.py:28
  16.0 162.1 %all-gather.17.cloned.1.call-start = ((), (), s32[]{:S(2)}) async-start(), calls=%async_computation.14 | async-start | bytes 9830400 | tf_op jit(solution)/shard_map/all_gather | solution.py:28
  20.3 209.5 %all-gather.21.cloned.1.call-start = ((), (), s32[]{:S(2)}) async-start(), calls=%async_computation.16 | async-start | bytes 9830400 | tf_op jit(solution)/shard_map/all_gather | solution.py:28
  20.9 263.6 %all-gather.23.cloned.1.call-start = ((), (), s32[]{:S(2)}) async-start(), calls=%async_computation.17 | async-start | bytes 9830400 | tf_op jit(solution)/shard_map/all_gather | solution.py:28
  21.5 317.7 %all-gather.19.cloned.1.call-start = ((), (), s32[]{:S(2)}) async-start(), calls=%async_computation.15 | async-start | bytes 9830400 | tf_op jit(solution)/shard_map/all_gather | solution.py:28
  22.1 855.6 %reduce-scatter.15.cloned.1.call-start = ((), (), s32[]{:S(2)}) async-start(), calls=%async_computation.10 | async-start | bytes 9830400 | tf_op jit(solution)/shard_map/reduce_scatter | solution.py:31
  43.1 78.4 %copy-start.3 = (f32[4096]{0:T(1024)}, f32[4096]{0:T(1024)S(1)}, u32[]{:S(2)}) copy-start(f32[4096]{0:T(1024)S(1)} %fusion.57) | copy-start | bytes 49156
  220.2 119.0 %copy-start.7 = (f32[4096]{0:T(1024)}, f32[4096]{0:T(1024)S(1)}, u32[]{:S(2)}) copy-start(f32[4096]{0:T(1024)S(1)} %fusion.58) | copy-start | bytes 49156
  446.3 48.5 %copy-start.11 = (f32[4096]{0:T(1024)S(1)}, f32[4096]{0:T(1024)}, u32[]{:S(2)}) copy-start(f32[4096]{0:T(1024)} %copy-done.10) | copy-start | bytes 49156
  446.3 48.5 %copy-start = (bf16[1,4096,1280]{1,2,0:T(8,128)(2,1)S(1)}, bf16[1,4096,1280]{1,2,0:T(8,128)(2,1)}, u32[]{:S(2)}) copy-start(bf16[1,4096,1280]{1,2,0:T(8,128)(2,1)} %copy.9) | copy-start | bytes 31457284
  446.3 48.5 %copy-start.8 = (f32[4096]{0:T(1024)S(1)}, f32[4096]{0:T(1024)}, u32[]{:S(2)}) copy-start(f32[4096]{0:T(1024)} %copy-done.7) | copy-start | bytes 49156
  550.0 327.7 %reduce-scatter.17.cloned.1.call-start = ((), (), s32[]{:S(2)}) async-start(), calls=%async_computation.11 | async-start | bytes 9830400 | tf_op jit(solution)/shard_map/reduce_scatter | solution.py:31
  597.0 280.7 %reduce-scatter.11.cloned.1.call-start = ((), (), s32[]{:S(2)}) async-start(), calls=%async_computation.8 | async-start | bytes 9830400 | tf_op jit(solution)/shard_map/reduce_scatter | solution.py:31
  597.1 72.8 %copy-start.4 = (f32[4096]{0:T(1024)S(1)}, f32[4096]{0:T(1024)}, u32[]{:S(2)}) copy-start(f32[4096]{0:T(1024)} %copy-done.3) | copy-start | bytes 49156
  713.4 164.3 %reduce-scatter.13.cloned.1.call-start = ((), (), s32[]{:S(2)}) async-start(), calls=%async_computation.9 | async-start | bytes 9830400 | tf_op jit(solution)/shard_map/reduce_scatter | solution.py:31
  756.8 144.9 %reduce-scatter.9.cloned.1.call-start = ((), (), s32[]{:S(2)}) async-start(), calls=%async_computation.7 | async-start | bytes 9830400 | tf_op jit(solution)/shard_map/reduce_scatter | solution.py:31
  797.1 168.0 %reduce-scatter.7.cloned.1.call-start = ((), (), s32[]{:S(2)}) async-start(), calls=%async_computation.6 | async-start | bytes 9830400 | tf_op jit(solution)/shard_map/reduce_scatter | solution.py:31
  837.3 396.4 %all-reduce.3.cloned.1.call-start = ((), (), s32[]{:S(2)}) async-start(), calls=%async_computation.18 | async-start | bytes 23592960 | tf_op jit(solution)/shard_map/psum | solution.py:31
  965.1 48.5 %slice-start = ((s8[10485760]{0:T(1024)(128)(4,1)}), s8[2097152]{0:T(1024)(128)(4,1)S(1)}, s32[]{:S(2)}) async-start(s8[10485760]{0:T(1024)(128)(4,1)} %bitcast.84), calls=%async_computation.19 | async-start | bytes 4194304
  965.2 48.4 %copy-start.2 = (f32[4096]{0:T(1024)S(1)}, f32[4096]{0:T(1024)}, u32[]{:S(2)}) copy-start(f32[4096]{0:T(1024)} %copy-done.1) | copy-start | bytes 49156
  965.2 48.5 %slice-start.1 = ((s8[10485760]{0:T(1024)(128)(4,1)}), s8[4194304]{0:T(1024)(128)(4,1)S(1)}, s32[]{:S(2)}) async-start(s8[10485760]{0:T(1024)(128)(4,1)} %bitcast.84), calls=%async_computation.20 | async-start | bytes 8388608
  965.2 48.5 %slice-start.2 = ((s8[10485760]{0:T(1024)(128)(4,1)}), s8[4194304]{0:T(1024)(128)(4,1)S(1)}, s32[]{:S(2)}) async-start(s8[10485760]{0:T(1024)(128)(4,1)} %bitcast.84), calls=%async_computation.21 | async-start | bytes 8388608
  965.2 48.5 %copy-start.6 = (f32[4096]{0:T(1024)S(1)}, f32[4096]{0:T(1024)}, u32[]{:S(2)}) copy-start(f32[4096]{0:T(1024)} %copy-done.3) | copy-start | bytes 49156
  (4 other events, 85.2 us)
Sparse Core Ops, SparseCore 0:
  11.7 55.5 all-gather.12
  68.8 52.6 all-gather.14
  123.0 52.6 all-gather.16
  177.1 52.6 all-gather.20
  231.8 52.6 all-gather.22
  286.5 52.6 all-gather.18
  550.1 61.0 reduce-scatter.14
  613.7 61.0 reduce-scatter.16
  713.6 61.0 reduce-scatter.10
  777.0 61.0 reduce-scatter.12
  840.6 61.0 reduce-scatter.8
  904.1 61.0 reduce-scatter.6
  968.0 265.6 all-reduce.2
where the time goes:
time: 1260 us; the launch traced here: 1250 us
  matrix products  794 us (63%)
  waiting for transfers between devices  338 us (27%)
  local copies, waits for them, and re-layouts  57.8 us (5%)
  other arithmetic  45.5 us (4%)
  between operations  14.5 us (1%)
    dot_general x6, matrix products, layer(): up = jnp.dot(a, w['w_up'], preferred_element_type=jnp.float32)  282 us
    dot_general x6, matrix products, layer(): gate = jnp.dot(a, w['w_gate'], preferred_element_type=jnp.float32)  270 us
    dot_general x5, matrix products, matmul(): jnp.dot(a, w, preferred_element_type=jnp.float32).astype(jnp.bfloat16)  242 us
    psum x1, waiting for transfers between devices, summed(): lax.psum(lax.psum_scatter(term, 's', scatter_dimension=0, tiled=True), 'r')  191 us
    reduce_scatter x6, waiting for transfers between devices, summed(): lax.psum_scatter(term, 's', scatter_dimension=0, tiled=True)  87.4 us
    all_gather x6, waiting for transfers between devices, fetched(): lax.all_gather(w[number], 's', axis=0, tiled=True)  58.7 us
    unnamed x33, local copies, waits for them, and re-layouts  44.9 us
  transfers between devices with their start and end apart: 13, of which 8 were waited for; matrix products, arithmetic and copies ran while one was open for 54% of the time, Pallas kernels for 0%

commit v1 on v0

v1 whole, which is shorter than its diff:
```python
import jax
import jax.numpy as jnp
from jax import lax
from jax.experimental import pallas as pl
from jax.experimental.pallas import tpu as pltpu
from jax.sharding import PartitionSpec as P

F32, BF16 = jnp.float32, jnp.bfloat16
ANY = pl.BlockSpec(memory_space=pl.ANY)
MESH = pl.DeviceIdType.MESH
NT = (((1,), (1,)), ((), ()))
TN = (((0,), (0,)), ((), ()))
CHUNKS = 4


def dot(a, b):
    return jnp.dot(a, b, preferred_element_type=F32)


def dot_nt(a, b):
    return lax.dot_general(a, b, NT, preferred_element_type=F32)


def dot_tn(a, b):
    return lax.dot_general(a, b, TN, preferred_element_type=F32)


def rounded(v):
    return v.astype(BF16).astype(F32)


def sigmoid(g):
    return pl.reciprocal(1.0 + jnp.exp(-g))


def normed(wide):
    return wide * lax.rsqrt(jnp.mean(wide * wide, -1, keepdims=True) + 1e-6)


def rows(tile, width):
    return pl.BlockSpec((tile, width), lambda i: (i, 0))


def shaped(*shape, dtype=BF16):
    return jax.ShapeDtypeStruct(shape, dtype)


class Place:
    def __init__(self):
        self.me, self.y = lax.axis_index("s"), lax.axis_index("r")
        x, c = self.me // 2, self.me % 2
        self.mate, self.far, self.far_mate = 2 * x + 1 - c, 2 * (1 - x) + c, 2 * (1 - x) + 1 - c
        self.to = {"mate": {"s": self.mate}, "x": {"s": self.far}, "y": {"r": 1 - self.y}}

    def greet(self, whom):
        barrier = pltpu.get_barrier_semaphore()
        for name in whom:
            pl.semaphore_signal(barrier, inc=1, device_id=self.to[name], device_id_type=MESH)
        pl.semaphore_wait(barrier, len(whom))


def part_rows(ref, start, size):
    return ref.at[pl.ds(pl.multiple_of(start, 16), size)]


def params(collective=None):
    more = {} if collective is None else dict(collective_id=collective, has_side_effects=True)
    return pltpu.CompilerParams(dimension_semantics=("arbitrary",), vmem_limit_bytes=62 << 20, **more)


def cost(flops):
    return pl.CostEstimate(flops=flops, bytes_accessed=1 << 20, transcendentals=0)


class Unit:
    def __init__(self, name, layer, start, width):
        self.name, self.layer, self.start, self.width = name, layer, start, width


class Mover:
    KINDS = ("own", "x", "y", "straight", "around")

    def __init__(self, units, weights, buffers, send, recv):
        self.units, self.weights, self.buffers, self.send, self.recv = units, weights, buffers, send, recv
        self.at = Place()

    def copy(self, n, kind, arriving=False):
        unit, buf, at = self.units[n], self.buffers[n], self.at
        block = buf.shape[0] // 4
        half = block // 2
        w = self.weights[unit.name].at[unit.layer]
        cols = pl.ds(unit.start, unit.width)
        mine, other = at.y * half, (1 - at.y) * half
        if arriving:
            start, size = {
                "own": (at.mate * block, block),
                "x": (at.far * block + mine, half),
                "y": (at.far * block + other, half),
                "straight": (at.far_mate * block + mine, half),
                "around": (at.far_mate * block + other, half),
            }[kind]
            src = dst = part_rows(buf, start, size)
        elif kind == "own":
            src, dst = w.at[:, cols], part_rows(buf, at.me * block, block)
        elif kind == "x":
            src, dst = w.at[pl.ds(pl.multiple_of(mine, 16), half), cols], part_rows(buf, at.me * block + mine, half)
        else:
            src = dst = part_rows(buf, at.far * block + (other if kind == "around" else mine), half)
        k = self.KINDS.index(kind)
        to = at.to[{"x": "x", "y": "y"}.get(kind, "mate")]
        return pltpu.make_async_remote_copy(src, dst, self.send.at[n, k], self.recv.at[n, k], device_id=to, device_id_type=MESH)

    def start(self, ns, *kinds):
        for n in ns:
            for kind in kinds:
                self.copy(n, kind).start()

    def arrived(self, ns, *kinds):
        for n in ns:
            for kind in kinds:
                self.copy(n, kind, arriving=True).wait_recv()

    def sent(self, ns):
        for n in ns:
            for kind in self.KINDS:
                self.copy(n, kind).wait_send()


def load(pairs, sems, first=0):
    at, made = Place(), []
    for units, scratch in pairs:
        col = 0
        for unit, w, buf in units:
            block = buf.shape[0] // 4
            for n, who in enumerate((at.me, at.mate, at.far, at.far_mate)):
                src = w.at[unit.layer, :, pl.ds(unit.start, unit.width)] if n == 0 else part_rows(buf, who * block, block)
                dst = scratch.at[pl.ds(pl.multiple_of(who * block, 16), block), pl.ds(col, unit.width)]
                made.append(pltpu.make_async_copy(src, dst, sems.at[first + len(made)]))
                made[-1].start()
            col += unit.width
    return made


class Whole:
    def __init__(self, w, units, buffers):
        self.w, self.units, self.buffers = w, units, buffers
        self.operands = [w, *buffers]
        self.shape = (4 * w.shape[1], w.shape[2])
        self.copies = 4 * len(units)

    def pairs(self, refs):
        return [(unit, refs[0], buf) for unit, buf in zip(self.units, refs[1:], strict=True)]


def fetch(matrices, refs, scratches, sems):
    @pl.when(pl.program_id(0) == 0)
    def _():
        pairs, used = [], 0
        for matrix, scratch in zip(matrices, scratches, strict=True):
            count = len(matrix.operands)
            pairs.append((matrix.pairs(refs[used : used + count]), scratch))
            used += count
        for copy in load(pairs, sems):
            copy.wait()


class Sends:
    def __init__(self, *items):
        self.items = items
        self.arrays = [array for array, _ in items]
        self.out_shape = [shaped(2, array.shape[0] // 4, array.shape[1]) if to == "term" else shaped(*array.shape) for array, to in items]
        self.count = sum(2 if to == "term" else 1 for _, to in items)
        self.scratch = [pltpu.SemaphoreType.DMA((self.count,))] * 2 if items else []
        self.whom = sorted({"mate" if to == "term" else to for _, to in items})

    def copies(self, at, sources, targets, send, recv):
        made = []
        for (array, to), src, dst in zip(self.items, sources, targets, strict=True):
            pairs = [(src, dst)]
            if to == "term":
                block = array.shape[0] // 4
                pairs = [(part_rows(src, at.mate * block, block), dst.at[0]), (part_rows(src, at.far_mate * block, block), dst.at[1])]
            for s, d in pairs:
                n = len(made)
                made.append(pltpu.make_async_remote_copy(s, d, send.at[n], recv.at[n], device_id=at.to["mate" if to == "term" else to], device_id_type=MESH))
        return made


IDS = {"gate_up": 0, "down": 1}


def hosted(kernel, grid, flops, operands, in_specs, out_specs, out_shape, scratch, sends, after, name, aliases=None):
    ins, outs, count = len(operands), len(out_shape), len(sends.items)
    collective = IDS.setdefault(name, len(IDS)) if count else None

    def body(*refs):
        own_in, sources, rest = refs[:ins], refs[ins : ins + count], refs[ins + count + 1 :]
        own_out, targets, rest = rest[:outs], rest[outs : outs + count], rest[outs + count :]
        own_scratch, sems = rest[: len(scratch)], rest[len(scratch) :]
        step = pl.program_id(0)
        if count:

            @pl.when(step == 0)
            def _():
                at = Place()
                at.greet(sends.whom)
                for copy in sends.copies(at, sources, targets, *sems):
                    copy.start()

        kernel(*own_in, *own_out, *own_scratch)
        if count:

            @pl.when(step == grid - 1)
            def _():
                for copy in sends.copies(Place(), sources, targets, *sems):
                    copy.wait()

    results = pl.pallas_call(
        body,
        grid=(grid,),
        cost_estimate=cost(flops),
        compiler_params=params(collective),
        in_specs=list(in_specs) + [ANY] * (count + 1),
        out_specs=list(out_specs) + [ANY] * count,
        out_shape=list(out_shape) + sends.out_shape,
        scratch_shapes=list(scratch) + sends.scratch,
        input_output_aliases=aliases or {},
        name=name,
    )(*operands, *sends.arrays, after)
    return results[:outs], results[outs:]


def first_kernel(x, weights):
    tokens, d = x.shape
    ff = weights["g"].shape[2]
    width, tile = ff // CHUNKS, min(512, tokens)
    tiles = tokens // tile
    part = min(256, width)
    units = []
    for c in range(CHUNKS):
        units += [Unit("g", 0, c * width, width), Unit("u", 0, c * width, width)]
    groups = [(2 * c, 2 * c + 1) for c in range(CHUNKS)]
    for name, layer, which in (("d", 0, (0, 1)), ("g", 1, (0, 1)), ("u", 1, (0,))):
        columns = weights[name].shape[2] // 2
        for n in which:
            groups.append((len(units),))
            units.append(Unit(name, layer, n * columns, columns))
    names = list(weights)
    total_steps = CHUNKS * tiles
    def step_of(time):
        return max(0, int((time - 29.0) / 2.55) + 1)

    events = {}
    for k in range(len(groups)):
        if k >= 2:
            events.setdefault(min(step_of(11.0 * (k + 1) + 3), total_steps - 1), []).append(("x", k))
        if k >= 1:
            events.setdefault(min(step_of(11.0 * (k + 2) + 6), total_steps - 1), []).append(("y", k))

    def kernel(x_ref, *refs):
        w_refs = dict(zip(names, refs[:3], strict=True))
        s_ref, q_ref, h_ref, a_ref = refs[3:7]
        buffers = refs[7 : 7 + len(units)]
        normal, wg, wu, load_sems, send, recv = refs[7 + len(units) :]
        step = pl.program_id(0)
        chunk, row = step // tiles, step % tiles
        move = Mover(units, w_refs, buffers, send, recv)

        def over_x(k):
            move.arrived(groups[k], "x")
            move.start(groups[k], "y", "straight")
            if k + 2 < len(groups):
                move.start(groups[k + 2], "x")

        def over_y(k):
            move.arrived(groups[k], "y")
            move.start(groups[k], "around")

        @pl.when(step == 0)
        def _():
            move.at.greet(("mate", "x", "y"))
            move.start(groups[0], "x")
            move.start(groups[1], "x")
            for group in groups:
                move.start(group, "own")

        @pl.when(chunk == 0)
        def _():
            a_ref[...] = normal[pl.ds(pl.multiple_of(row * tile, tile), tile)] = normed(x_ref[...].astype(F32)).astype(BF16)

        @pl.when(step == 0)
        def _():
            over_x(0)
            over_x(1)
            over_y(0)

        for at, these in events.items():

            @pl.when(step == at)
            def _():
                for kind, k in these:
                    (over_x if kind == "x" else over_y)(k)

        for c in range(CHUNKS):

            @pl.when(step == c * tiles)
            def _():
                move.arrived(groups[c], "own", "straight", "around")
                pairs = [([(units[n], w_refs[units[n].name], buffers[n])], scratch) for n, scratch in zip(groups[c], (wg, wu), strict=True)]
                for copy in load(pairs, load_sems):
                    copy.wait()

        av = normal[pl.ds(pl.multiple_of(row * tile, tile), tile)]
        for j in range(0, width, part):
            at = pl.ds(j, part)
            g, u = dot(av, wg[:, at]), dot(av, wu[:, at])
            s = sigmoid(g)
            sl = g * s
            s_ref[:, at] = sl
            q_ref[:, at] = u * (s + sl * (1.0 - s))
            h_ref[:, at] = (sl * u).astype(BF16)

        @pl.when(step == total_steps - 1)
        def _():
            for k in range(CHUNKS, len(groups)):
                move.arrived(groups[k], "own", "straight", "around")
            move.sent(range(len(units)))

    once = pl.BlockSpec((tile, d), lambda i: (jnp.minimum(i, tiles - 1), 0))
    out = pl.BlockSpec((tile, width), lambda i: (i % tiles, i // tiles))
    results = pl.pallas_call(
        kernel,
        grid=(total_steps,),
        cost_estimate=cost(4 * tokens * d * ff),
        compiler_params=params(0),
        in_specs=[once] + [ANY] * 3,
        out_specs=[out] * 3 + [once] + [ANY] * len(units),
        out_shape=[shaped(tokens, ff, dtype=F32)] * 2
        + [shaped(tokens, ff), shaped(tokens, d)]
        + [shaped(4 * weights[unit.name].shape[1], unit.width) for unit in units],
        scratch_shapes=[pltpu.VMEM((tokens, d), BF16)]
        + [pltpu.VMEM((d, width), BF16)] * 2
        + [pltpu.SemaphoreType.DMA((8,)), pltpu.SemaphoreType.DMA((len(units), 5)), pltpu.SemaphoreType.DMA((len(units), 5))],
        name="gate_up",
    )(x, *weights.values())
    kept, buffers = results[:4], results[4:]
    gathered = {}
    for unit, buf in zip(units, buffers, strict=True):
        gathered.setdefault((unit.name, unit.layer), []).append((unit, buf))
    return kept, gathered


def second_kernel(hidden, h, w, weights):
    tokens, ff = hidden.shape
    d = h.shape[1]
    tile = min(256, tokens)
    steps = tokens // tile
    half_u, half_d = weights["u"].shape[2] // 2, weights["d"].shape[2] // 2
    units = [Unit("u", 1, half_u, half_u), Unit("d", 1, 0, half_d), Unit("d", 1, half_d, half_d)]
    names = ("u", "d")
    events = {5: [("x", 0)], 9: [("x", 1)], 10: [("y", 0)], 13: [("x", 2)], 14: [("y", 1)], 15: [("y", 2)]}
    events = {min(at, steps - 1): these for at, these in events.items()} if steps >= 16 else {steps - 1: [(kind, k) for k in range(3) for kind in "xy"]}
    count = len(w.operands)

    def kernel(hidden_ref, h_ref, *refs):
        ins, refs = refs[:count], refs[count:]
        w_refs = dict(zip(names, refs[:2], strict=True))
        o_ref, a_ref = refs[2:4]
        buffers = refs[4:7]
        wd, load_sems, send, recv = refs[7:]
        step = pl.program_id(0)
        move = Mover(units, w_refs, buffers, send, recv)

        @pl.when(step == 0)
        def _():
            move.at.greet(("mate", "x", "y"))
            move.start((0, 1), "x")
            move.start(range(3), "own")

        fetch((w,), ins, (wd,), load_sems)
        out = (h_ref[...].astype(F32) + rounded(dot(hidden_ref[...], wd[...]))).astype(BF16)
        o_ref[...] = out
        a_ref[...] = normed(out.astype(F32)).astype(BF16)

        for at, these in events.items():

            @pl.when(step == at)
            def _():
                for kind, k in these:
                    if kind == "x":
                        move.arrived((k,), "x")
                        move.start((k,), "y", "straight")
                        if k == 0:
                            move.start((2,), "x")
                    else:
                        move.arrived((k,), "y")
                        move.start((k,), "around")

        @pl.when(step == steps - 1)
        def _():
            move.arrived(range(3), "own", "straight", "around")
            move.sent(range(3))

    results = pl.pallas_call(
        kernel,
        grid=(steps,),
        cost_estimate=cost(2 * tokens * d * ff),
        compiler_params=params(1),
        in_specs=[rows(tile, ff), rows(tile, d)] + [ANY] * (count + 2),
        out_specs=[rows(tile, d)] * 2 + [ANY] * 3,
        out_shape=[shaped(tokens, d)] * 2 + [shaped(4 * weights[unit.name].shape[1], unit.width) for unit in units],
        scratch_shapes=[
            pltpu.VMEM((ff, d), BF16),
            pltpu.SemaphoreType.DMA((w.copies,)),
            pltpu.SemaphoreType.DMA((3, 5)),
            pltpu.SemaphoreType.DMA((3, 5)),
        ],
        name="down",
    )(hidden, h, *w.operands, weights["u"], weights["d"])
    return results[:2], list(zip(units, results[2:], strict=True))


def scratch_for(*matrices):
    return [pltpu.VMEM(m.shape, BF16) for m in matrices] + [pltpu.SemaphoreType.DMA((sum(m.copies for m in matrices),))]


def operands_of(*matrices):
    return [operand for m in matrices for operand in m.operands]


def last_layer(a, dy, gate, up, w):
    tokens, d = a.shape
    ff = gate.shape[1]
    tile, part = min(256, tokens), 256
    matrices = (gate, up, w)
    weights = operands_of(*matrices)

    def kernel(a_ref, dy_ref, *refs):
        ins, (h_ref, dg_ref, du_ref, wg, wu, wd, sems) = refs[: len(weights)], refs[len(weights) :]
        fetch(matrices, ins, (wg, wu, wd), sems)
        av, dyv = a_ref[...], dy_ref[...]
        for j in range(0, ff, part):
            at = pl.ds(j, part)
            g, u, dh = dot(av, wg[:, at]), dot(av, wu[:, at]), rounded(dot_nt(dyv, wd[at, :]))
            s = sigmoid(g)
            sl = g * s
            h_ref[:, at] = (sl * u).astype(BF16)
            dg_ref[:, at] = (dh * (u * (s + sl * (1.0 - s)))).astype(BF16)
            du_ref[:, at] = (dh * sl).astype(BF16)

    return hosted(
        kernel,
        tokens // tile,
        6 * tokens * d * ff,
        [a, dy, *weights],
        [rows(tile, d)] * 2 + [ANY] * len(weights),
        [rows(tile, ff)] * 3,
        [shaped(tokens, ff)] * 3,
        scratch_for(*matrices),
        Sends(),
        a,
        "last_layer",
    )[0]


def hidden_back(dy, silu, slope, w, sends, after):
    tokens, d = dy.shape
    ff = silu.shape[1]
    tile, part = min(256, tokens), 256
    weights = w.operands

    def kernel(dy_ref, s_ref, q_ref, *refs):
        ins, (dg_ref, du_ref, wd, sems) = refs[: len(weights)], refs[len(weights) :]
        fetch((w,), ins, (wd,), sems)
        dyv = dy_ref[...]
        for j in range(0, ff, part):
            at = pl.ds(j, part)
            dh = rounded(dot_nt(dyv, wd[at, :]))
            dg_ref[:, at] = (dh * q_ref[:, at]).astype(BF16)
            du_ref[:, at] = (dh * s_ref[:, at]).astype(BF16)

    return hosted(
        kernel,
        tokens // tile,
        2 * tokens * d * ff,
        [dy, silu, slope, *weights],
        [rows(tile, d)] + [rows(tile, ff)] * 2 + [ANY] * len(weights),
        [rows(tile, ff)] * 2,
        [shaped(tokens, ff)] * 2,
        scratch_for(w),
        sends,
        after,
        "hidden_back",
    )


def norm_back(da, wide, dres):
    scale = lax.rsqrt(jnp.mean(wide * wide, -1, keepdims=True) + 1e-6)
    along = jnp.sum(da * wide, -1, keepdims=True) * (scale * scale * scale) * (1.0 / wide.shape[-1])
    return (dres + rounded(da * scale - wide * along)).astype(BF16)


def input_back(dg, du, h, dres, gate, up, sends, after):
    tokens, ff = dg.shape
    d = h.shape[1]
    tile = min(256, tokens)
    weights = operands_of(gate, up)

    def kernel(dg_ref, du_ref, h_ref, r_ref, *refs):
        ins, (o_ref, wg, wu, sems) = refs[: len(weights)], refs[len(weights) :]
        fetch((gate, up), ins, (wg, wu), sems)
        da = rounded(rounded(dot_nt(dg_ref[...], wg[...])) + rounded(dot_nt(du_ref[...], wu[...])))
        o_ref[...] = norm_back(da, h_ref[...].astype(F32), r_ref[...].astype(F32))

    return hosted(
        kernel,
        tokens // tile,
        4 * tokens * d * ff,
        [dg, du, h, dres, *weights],
        [rows(tile, ff)] * 2 + [rows(tile, d)] * 2 + [ANY] * len(weights),
        [rows(tile, d)],
        [shaped(tokens, d)],
        scratch_for(gate, up),
        sends,
        after,
        "input_back",
    )


def input_back_gate(dg, gate, part, parts, sends, after):
    tokens, ff = dg.shape[0] // parts, dg.shape[1]
    d = gate.shape[0]
    tile = min(256, tokens)
    first = part * (tokens // tile)
    weights = gate.operands

    def kernel(dg_ref, *refs):
        ins, (o_ref, wg, sems) = refs[: len(weights)], refs[len(weights) :]
        fetch((gate,), ins, (wg,), sems)
        o_ref[...] = dot_nt(dg_ref[...], wg[...]).astype(BF16)

    return hosted(
        kernel,
        tokens // tile,
        2 * tokens * d * ff,
        [dg, *weights],
        [pl.BlockSpec((tile, ff), lambda i: (i + first, 0))] + [ANY] * len(weights),
        [rows(tile, d)],
        [shaped(tokens, d)],
        scratch_for(gate),
        sends,
        after,
        f"input_back_gate_{part}",
    )


def input_back_up(du, from_gate, h, dres, up, sends, after):
    tokens, ff = du.shape
    d = h.shape[1]
    tile = min(256, tokens)
    split = (tokens // tile) // 2
    weights = up.operands

    def kernel(du_ref, f0_ref, f1_ref, h_ref, r_ref, *refs):
        ins, (o_ref, wu, sems) = refs[: len(weights)], refs[len(weights) :]
        fetch((up,), ins, (wu,), sems)
        first = jnp.where(pl.program_id(0) < split, f0_ref[...].astype(F32), f1_ref[...].astype(F32))
        da = rounded(first + rounded(dot_nt(du_ref[...], wu[...])))
        o_ref[...] = norm_back(da, h_ref[...].astype(F32), r_ref[...].astype(F32))

    return hosted(
        kernel,
        tokens // tile,
        2 * tokens * d * ff,
        [du, *from_gate, h, dres, *weights],
        [
            rows(tile, ff),
            pl.BlockSpec((tile, d), lambda i: (jnp.minimum(i, split - 1), 0)),
            pl.BlockSpec((tile, d), lambda i: (jnp.maximum(i - split, 0), 0)),
            rows(tile, d),
            rows(tile, d),
        ]
        + [ANY] * len(weights),
        [rows(tile, d)],
        [shaped(tokens, d)],
        scratch_for(up),
        sends,
        after,
        "input_back_up",
    )


def whole_block(shape):
    return pl.BlockSpec(shape, lambda i: (0, 0), pipeline_mode=pl.Buffered(1))


def grad_in(a, b, sends, after, name, part=0, parts=1):
    tokens, d = a.shape
    width = b.shape[1] // parts
    tile = min(512, width)
    first = part * (width // tile)

    def kernel(a_ref, b_ref, o_ref):
        o_ref[...] = dot_tn(a_ref[...], b_ref[...]).astype(BF16)

    (term,), arrived = hosted(
        kernel,
        width // tile,
        2 * tokens * d * width,
        [a, b],
        [whole_block((tokens, d)), pl.BlockSpec((tokens, tile), lambda i: (0, i + first))],
        [pl.BlockSpec((d, tile), lambda i: (0, i))],
        [shaped(d, width)],
        [],
        sends,
        after,
        name,
    )
    return term, arrived


def grad_out(hidden, dy, sends, after, name):
    tokens, d = dy.shape
    ff = hidden.shape[1]
    tile = min(512, ff)

    def kernel(hidden_ref, dy_ref, o_ref):
        o_ref[...] = dot_tn(hidden_ref[...], dy_ref[...]).astype(BF16)

    (term,), arrived = hosted(
        kernel,
        ff // tile,
        2 * tokens * d * ff,
        [hidden, dy],
        [pl.BlockSpec((tokens, tile), lambda i: (0, i)), whole_block((tokens, d))],
        [rows(tile, d)],
        [shaped(ff, d)],
        [],
        sends,
        after,
        name,
    )
    return term, arrived


def total(*terms):
    return sum(t.astype(F32) for t in terms).astype(BF16)


def solution(mesh):
    def block_of(term, which):
        size = term.shape[0] // 4
        return lax.dynamic_slice_in_dim(term, which * size, size, 0)

    def step(x, dy, w_gate, w_up, w_down):
        x, dy = x[0], dy[0]
        weights = {"g": w_gate, "u": w_up, "d": w_down}
        me = lax.axis_index("s")
        far = (me + 2) % 4

        (silu, slope, hidden0, a0), gathered = first_kernel(x, weights)

        def whole(name, layer):
            units, buffers = zip(*gathered[name, layer], strict=True)
            return Whole(weights[name], units, buffers)

        gate0, up0, down0 = (whole(name, 0) for name in "gud")
        (h1, a1), rest = second_kernel(hidden0, x, down0, weights)
        for unit, buf in rest:
            gathered.setdefault((unit.name, unit.layer), []).append((unit, buf))
        gate1, up1, down1 = (whole(name, 1) for name in "gud")
        hidden1, dg1, du1 = last_layer(a1, dy, gate1, up1, down1)

        def for_x(term, received):
            return total(block_of(term, far), received[1])

        def for_y(term, received, over_x):
            return total(block_of(term, me), received[0], over_x)

        wd1, _ = grad_out(hidden1, dy, Sends(), dy, "wd1")
        wg1, (r_wd1,) = grad_in(a1, dg1, Sends((wd1, "term")), dy, "wg1")
        wu1, (x_wd1, r_wg1) = grad_in(a1, du1, Sends((for_x(wd1, r_wd1), "x"), (wg1, "term")), dy, "wu1")
        s_wd1 = for_y(wd1, r_wd1, x_wd1)
        (dh,), (y_wd1, x_wg1, r_wu1) = input_back(dg1, du1, h1, dy, gate1, up1, Sends((s_wd1, "y"), (for_x(wg1, r_wg1), "x"), (wu1, "term")), dy)
        s_wg1 = for_y(wg1, r_wg1, x_wg1)
        wd0, (y_wg1, x_wu1) = grad_out(hidden0, dh, Sends((s_wg1, "y"), (for_x(wu1, r_wu1), "x")), dh, "wd0")
        s_wu1 = for_y(wu1, r_wu1, x_wu1)
        (dg0, du0), (y_wu1, r_wd0) = hidden_back(dh, silu, slope, down0, Sends((s_wu1, "y"), (wd0, "term")), dh)
        wg0, (x_wd0,) = grad_in(a0, dg0, Sends((for_x(wd0, r_wd0), "x")), dh, "wg0")
        s_wd0 = for_y(wd0, r_wd0, x_wd0)
        wu0, (y_wd0, r_wg0) = grad_in(a0, du0, Sends((s_wd0, "y"), (wg0, "term")), dh, "wu0")
        (b0,), (x_wg0, r_wu0) = input_back_gate(dg0, gate0, 0, 2, Sends((for_x(wg0, r_wg0), "x"), (wu0, "term")), dh)
        s_wg0 = for_y(wg0, r_wg0, x_wg0)
        (b1,), (y_wg0, x_wu0) = input_back_gate(dg0, gate0, 1, 2, Sends((s_wg0, "y"), (for_x(wu0, r_wu0), "x")), b0)
        s_wu0 = for_y(wu0, r_wu0, x_wu0)
        (dx,), (y_wu0,) = input_back_up(du0, (b0, b1), x, dh, up0, Sends((s_wu0, "y")), b1)

        return (
            dx[None],
            jnp.stack([total(s_wg0, y_wg0), total(s_wg1, y_wg1)]),
            jnp.stack([total(s_wu0, y_wu0), total(s_wu1, y_wu1)]),
            jnp.stack([total(s_wd0, y_wd0), total(s_wd1, y_wd1)]),
        )

    states, cut = P(("rep", "r", "s"), None, None), P(None, "s", None)
    return jax.shard_map(
        step,
        mesh=mesh,
        in_specs=(states, states) + (cut,) * 3,
        out_specs=(states,) + (P("rep", "s", None),) * 3,
        check_vma=False,
    )
```

time: 1260 us -> 993 us (0.79)
  Pallas kernels: 0 us -> 907 us
  matrix products: 794 us -> 0 us
  waiting for transfers between devices: 338 us -> 0 us
  local copies, waits for them, and re-layouts: 57.8 us -> 12.7 us
  other arithmetic: 45.5 us -> 64.5 us
  between operations: 14.5 us -> 1.33 us
    pallas_call x0 -> x14, Pallas kernels: none -> 907 us  [the longest x12 703 us: hosted(): pl.pallas_call(body, grid=(grid,), cost_estimate=cost(flops), compiler_pa...]
    dot_general x17 -> x0, matrix products: 794 us -> none  [the longest x6 282 us: layer(): up = jnp.dot(a, w['w_up'], preferred_element_type=jnp.float32)]
    psum x1 -> x0, waiting for transfers between devices: 191 us -> none  [summed(): lax.psum(lax.psum_scatter(term, 's', scatter_dimension=0, tiled=True), 'r')]
    reduce_scatter x6 -> x0, waiting for transfers between devices: 87.4 us -> none  [summed(): lax.psum_scatter(term, 's', scatter_dimension=0, tiled=True)]
    all_gather x6 -> x0, waiting for transfers between devices: 58.7 us -> none  [fetched(): lax.all_gather(w[number], 's', axis=0, tiled=True)]
    convert_element_type x0 -> x11, other arithmetic: none -> 51.9 us  [total(): return sum((t.astype(F32) for t in terms)).astype(BF16)]
    unnamed x33 -> x25, local copies, waits for them, and re-layouts: 44.9 us -> 12.7 us
    add_any x1 -> x0, other arithmetic: 14.9 us -> none  [normed(): wide = h.astype(jnp.float32)]
  transfers between devices with their start and end apart: 13 -> 0, of which waited for: 8 -> 0; matrix products, arithmetic and copies ran while one was open for 54% -> 0% of each run, Pallas kernels for 0% -> 0%
where the time goes in v1:
time: 993 us; the launch traced here: 985 us
  Pallas kernels  907 us (91%)
  other arithmetic  64.5 us (6%)
  local copies, waits for them, and re-layouts  12.7 us (1%)
    pallas_call x12, Pallas kernels, hosted(): pl.pallas_call(body, grid=(grid,), cost_estimate=cost(flops), compiler_pa...  703 us
    pallas_call x1, Pallas kernels, first_kernel(): pl.pallas_call(kernel, grid=(total_steps,), cost_estimate=cost(4 * tokens...  146 us
    pallas_call x1, Pallas kernels, second_kernel(): pl.pallas_call(kernel, grid=(steps,), cost_estimate=cost(2 * tokens * d *...  58 us
    convert_element_type x11, other arithmetic, total(): return sum((t.astype(F32) for t in terms)).astype(BF16)  51.9 us

profile of v1, /device:TPU:0, one launch (start us, length us, event | category | flops | bytes accessed | tf_op | source)
XLA Modules:
  0.0 985.2 jit_solution(16483619867717960328)
XLA Ops:
  0.6 145.9 %gate_up.1 = (f32[4096,3072]{1,0:T(8,128)}, f32[4096,3072]{1,0:T(8,128)}, bf16[4096,3072]{1,0:T(8,128)(2,1)}, bf16[4096,1280]{1,0:T(8,128)(2,1)}, bf16[1280,768]...) custom-call(bf16[4096,1280]{1,0:T(8,128)(2,1)} %bitcast.59, ...), custom_call_target="tpu_custom_call" | custom-call | flops 64424509440 | bytes 1048576 | tf_op jit(solution)/shard_map/gate_up/pallas_call | solution.py:331
  146.6 58.0 %down.1 = (bf16[4096,1280]{1,0:T(8,128)(2,1)}, bf16[4096,1280]{1,0:T(8,128)(2,1)}, bf16[1280,1536]{1,0:T(8,128)(2,1)}, bf16[3072,640]{1,0:T(8,128)(2,1)}, bf16[3072,640]{1,0:T(8,128)(2,1)}) custom-call(bf16[4096,3072]{1,0:T(8,128)(2,1)} %get-tuple-element.58.hidden_ref.refs_0_, bf16[4096,1280]{1,0:T(8,128)(2,1)} %bitcast.60, bf16[2,768,1280]{2,1,0:T(8,128)(2,1)} %refs_3_.3, ...), custom_call_target="tpu_custom_call" | custom-call | flops 32212254720 | bytes 1048576 | tf_op jit(solution)/shard_map/down/pallas_call | solution.py:404
  204.5 116.2 %last_layer.1 = (bf16[4096,3072]{1,0:T(8,128)(2,1)}, bf16[4096,3072]{1,0:T(8,128)(2,1)}, bf16[4096,3072]{1,0:T(8,128)(2,1)}) custom-call(bf16[4096,1280]{1,0:T(8,128)(2,1)} %get-tuple-element.61.refs_0_.refs_11_, bf16[4096,1280]{1,0:T(8,128)(2,1)} %bitcast.52, bf16[2,320,3072]{2,1,0:T(8,128)(2,1)} %refs_1_.5, ...), custom_call_target="tpu_custom_call" | custom-call | flops 96636764160 | bytes 1048576 | tf_op jit(solution)/shard_map/last_layer/pallas_call | solution.py:218
  320.7 40.3 %wd1.1.refs_2_ = bf16[3072,1280]{1,0:T(8,128)(2,1)} custom-call(bf16[4096,3072]{1,0:T(8,128)(2,1)} %get-tuple-element.71.refs_0_, bf16[4096,1280]{1,0:T(8,128)(2,1)} %bitcast.53, bf16[4096,1280]{1,0:T(8,128)(2,1)} %bitcast.54), custom_call_target="tpu_custom_call" | custom-call | flops 32212254720 | bytes 1048576 | tf_op jit(solution)/shard_map/wd1/pallas_call | solution.py:218
  361.1 40.7 %wg1.1 = (bf16[1280,3072]{1,0:T(8,128)(2,1)}, bf16[2,768,1280]{2,1,0:T(8,128)(2,1)}) custom-call(bf16[4096,1280]{1,0:T(8,128)(2,1)} %get-tuple-element.61.refs_0_.refs_11_, bf16[4096,3072]{1,0:T(8,128)(2,1)} %get-tuple-element.68.refs_1_.refs_0_, bf16[3072,1280]{1,0:T(8,128)(2,1)} %wd1.1.refs_2_, bf16[4096,1280]{1,0:T(8,128)(2,1)} %bitcast.55), custom_call_target="tpu_custom_call" | custom-call | flops 32212254720 | bytes 1048576 | tf_op jit(solution)/shard_map/wg1/pallas_call | solution.py:218
  405.7 51.8 %wu1.1 = (bf16[1280,3072]{1,0:T(8,128)(2,1)}, bf16[768,1280]{1,0:T(8,128)(2,1)}, bf16[2,320,3072]{2,1,0:T(8,128)(2,1)}) custom-call(bf16[4096,1280]{1,0:T(8,128)(2,1)} %get-tuple-element.61.refs_0_.refs_11_, bf16[4096,3072]{1,0:T(8,128)(2,1)} %get-tuple-element.69.refs_1_, bf16[768,1280]{1,0:T(8,128)(2,1)} %fusion.15.refs_2_, ...), custom_call_target="tpu_custom_call" | custom-call | flops 32212254720 | bytes 1048576 | tf_op jit(solution)/shard_map/wu1/pallas_call | solution.py:218
  457.5 4.7 fusion.17.refs_10_
  462.2 4.1 fusion.14.refs_11_
  466.3 87.1 %input_back.1 = (bf16[4096,1280]{1,0:T(8,128)(2,1)}, bf16[768,1280]{1,0:T(8,128)(2,1)}, bf16[320,3072]{1,0:T(8,128)(2,1)}, bf16[2,320,3072]{2,1,0:T(8,128)(2,1)}) custom-call(bf16[4096,3072]{1,0:T(8,128)(2,1)} %get-tuple-element.68.refs_1_.refs_0_, bf16[4096,3072]{1,0:T(8,128)(2,1)} %get-tuple-element.69.refs_1_, ...), custom_call_target="tpu_custom_call" | custom-call | flops 64424509440 | bytes 1048576 | tf_op jit(solution)/shard_map/input_back/pallas_call | solution.py:218
  553.4 7.8 fusion.9
  561.2 50.9 %wd0.1 = (bf16[3072,1280]{1,0:T(8,128)(2,1)}, bf16[320,3072]{1,0:T(8,128)(2,1)}, bf16[320,3072]{1,0:T(8,128)(2,1)}) custom-call(bf16[4096,3072]{1,0:T(8,128)(2,1)} %get-tuple-element.58.hidden_ref.refs_0_, bf16[4096,1280]{1,0:T(8,128)(2,1)} %get-tuple-element.77.refs_1_.refs_4_.refs_0_.refs_8_.refs_3_, bf16[320,3072]{1,0:T(8,128)(2,1)} %get-tuple-element.113.refs_2_, ...), custom_call_target="tpu_custom_call" | custom-call | flops 32212254720 | bytes 1048576 | tf_op jit(solution)/shard_map/wd0/pallas_call | solution.py:218
  612.1 5.0 fusion.13.refs_6_
  617.1 67.1 %hidden_back.1 = (bf16[4096,3072]{1,0:T(8,128)(2,1)}, bf16[4096,3072]{1,0:T(8,128)(2,1)}, bf16[320,3072]{1,0:T(8,128)(2,1)}, bf16[2,768,1280]{2,1,0:T(8,128)(2,1)}) custom-call(bf16[4096,1280]{1,0:T(8,128)(2,1)} %get-tuple-element.77.refs_1_.refs_4_.refs_0_.refs_8_.refs_3_, f32[4096,3072]{1,0:T(8,128)} %get-tuple-element.78.refs_1_, ...), custom_call_target="tpu_custom_call" | custom-call | flops 32212254720 | bytes 1048576 | tf_op jit(solution)/shard_map/hidden_back/pallas_call | solution.py:218
  684.2 3.9 fusion.8.refs_2_
  688.1 50.8 %wg0.1 = (bf16[1280,3072]{1,0:T(8,128)(2,1)}, bf16[768,1280]{1,0:T(8,128)(2,1)}) custom-call(bf16[4096,1280]{1,0:T(8,128)(2,1)} %get-tuple-element.90.refs_0_, bf16[4096,3072]{1,0:T(8,128)(2,1)} %get-tuple-element.85.refs_1_.refs_0_, bf16[768,1280]{1,0:T(8,128)(2,1)} %fusion.8.refs_2_, ...), custom_call_target="tpu_custom_call" | custom-call | flops 32212254720 | bytes 1048576 | tf_op jit(solution)/shard_map/wg0/pallas_call | solution.py:218
  738.8 4.7 fusion.7.refs_2_
  743.6 50.8 %wu0.1 = (bf16[1280,3072]{1,0:T(8,128)(2,1)}, bf16[768,1280]{1,0:T(8,128)(2,1)}, bf16[2,320,3072]{2,1,0:T(8,128)(2,1)}) custom-call(bf16[4096,1280]{1,0:T(8,128)(2,1)} %get-tuple-element.90.refs_0_, bf16[4096,3072]{1,0:T(8,128)(2,1)} %get-tuple-element.84.refs_1_.refs_0_, bf16[768,1280]{1,0:T(8,128)(2,1)} %fusion.7.refs_2_, ...), custom_call_target="tpu_custom_call" | custom-call | flops 32212254720 | bytes 1048576 | tf_op jit(solution)/shard_map/wu0/pallas_call | solution.py:218
  794.3 4.1 fusion.5.refs_6_
  798.4 47.2 %input_back_gate_0.1 = (bf16[2048,1280]{1,0:T(8,128)(2,1)}, bf16[320,3072]{1,0:T(8,128)(2,1)}, bf16[2,320,3072]{2,1,0:T(8,128)(2,1)}) custom-call(bf16[4096,3072]{1,0:T(8,128)(2,1)} %get-tuple-element.85.refs_1_.refs_0_, bf16[2,320,3072]{2,1,0:T(8,128)(2,1)} %refs_1_.5, bf16[1280,768]{1,0:T(8,128)(2,1)} %get-tuple-element.86.refs_2_, ...), custom_call_target="tpu_custom_call" | custom-call | flops 16106127360 | bytes 1048576 | tf_op jit(solution)/shard_map/input_back_gate_0/pallas_call | solution.py:218
  845.6 5.1 fusion.4.refs_6_
  854.3 46.7 %input_back_gate_1.1 = (bf16[2048,1280]{1,0:T(8,128)(2,1)}, bf16[320,3072]{1,0:T(8,128)(2,1)}, bf16[320,3072]{1,0:T(8,128)(2,1)}) custom-call(bf16[4096,3072]{1,0:T(8,128)(2,1)} %get-tuple-element.85.refs_1_.refs_0_, bf16[2,320,3072]{2,1,0:T(8,128)(2,1)} %refs_1_.5, bf16[1280,768]{1,0:T(8,128)(2,1)} %get-tuple-element.86.refs_2_, ...), custom_call_target="tpu_custom_call" | custom-call | flops 16106127360 | bytes 1048576 | tf_op jit(solution)/shard_map/input_back_gate_1/pallas_call | solution.py:218
  901.0 5.0 fusion.1.refs_10_
  906.0 53.3 %input_back_up.1 = (bf16[4096,1280]{1,0:T(8,128)(2,1)}, bf16[320,3072]{1,0:T(8,128)(2,1)}) custom-call(bf16[4096,3072]{1,0:T(8,128)(2,1)} %get-tuple-element.84.refs_1_.refs_0_, bf16[2048,1280]{1,0:T(8,128)(2,1)} %get-tuple-element.96.refs_8_.refs_1_, bf16[2048,1280]{1,0:T(8,128)(2,1)} %get-tuple-element.99.refs_2_.refs_11_, bf16[4096,1280]{1,0:T(8,128)(2,1)} %bitcast.61, ...), custom_call_target="tpu_custom_call" | custom-call | flops 32212254720 | bytes 1048576 | tf_op jit(solution)/shard_map/input_back_up/pallas_call | solution.py:218
  976.0 8.7 copy.10
  (35 shorter events, 24.0 us)
Async XLA Ops:
  845.6 5.1 copy-start.6
  906.0 53.3 %copy-start.1 = (bf16[320,3072]{1,0:T(8,128)(2,1)S(1)}, bf16[320,3072]{1,0:T(8,128)(2,1)}, u32[]{:S(2)}) copy-start(bf16[320,3072]{1,0:T(8,128)(2,1)} %get-tuple-element.113.refs_2_) | copy-start | bytes 5898244
  959.3 2.4 copy-start.4
  959.3 2.7 copy-start.10
  962.8 2.4 copy-start
  962.8 3.5 copy-start.8
  965.1 1.9 copy-start.5
  965.1 2.5 copy-start.11
  968.3 2.4 copy-start.2
  968.3 3.5 copy-start.7
  970.7 1.9 copy-start.3
  970.7 2.5 copy-start.9

commit v2 on v1

--- a/solution.py
+++ b/solution.py
@@ -164,72 +164,6 @@
             copy.wait()
 
 
-class Sends:
-    def __init__(self, *items):
-        self.items = items
-        self.arrays = [array for array, _ in items]
-        self.out_shape = [shaped(2, array.shape[0] // 4, array.shape[1]) if to == "term" else shaped(*array.shape) for array, to in items]
-        self.count = sum(2 if to == "term" else 1 for _, to in items)
-        self.scratch = [pltpu.SemaphoreType.DMA((self.count,))] * 2 if items else []
-        self.whom = sorted({"mate" if to == "term" else to for _, to in items})
-
-    def copies(self, at, sources, targets, send, recv):
-        made = []
-        for (array, to), src, dst in zip(self.items, sources, targets, strict=True):
-            pairs = [(src, dst)]
-            if to == "term":
-                block = array.shape[0] // 4
-                pairs = [(part_rows(src, at.mate * block, block), dst.at[0]), (part_rows(src, at.far_mate * block, block), dst.at[1])]
-            for s, d in pairs:
-                n = len(made)
-                made.append(pltpu.make_async_remote_copy(s, d, send.at[n], recv.at[n], device_id=at.to["mate" if to == "term" else to], device_id_type=MESH))
-        return made
-
-
-IDS = {"gate_up": 0, "down": 1}
-
-
-def hosted(kernel, grid, flops, operands, in_specs, out_specs, out_shape, scratch, sends, after, name, aliases=None):
-    ins, outs, count = len(operands), len(out_shape), len(sends.items)
-    collective = IDS.setdefault(name, len(IDS)) if count else None
-
-    def body(*refs):
-        own_in, sources, rest = refs[:ins], refs[ins : ins + count], refs[ins + count + 1 :]
-        own_out, targets, rest = rest[:outs], rest[outs : outs + count], rest[outs + count :]
-        own_scratch, sems = rest[: len(scratch)], rest[len(scratch) :]
-        step = pl.program_id(0)
-        if count:
-
-            @pl.when(step == 0)
-            def _():
-                at = Place()
-                at.greet(sends.whom)
-                for copy in sends.copies(at, sources, targets, *sems):
-                    copy.start()
-
-        kernel(*own_in, *own_out, *own_scratch)
-        if count:
-
-            @pl.when(step == grid - 1)
-            def _():
-                for copy in sends.copies(Place(), sources, targets, *sems):
-                    copy.wait()
-
-    results = pl.pallas_call(
-        body,
-        grid=(grid,),
-        cost_estimate=cost(flops),
-        compiler_params=params(collective),
-        in_specs=list(in_specs) + [ANY] * (count + 1),
-        out_specs=list(out_specs) + [ANY] * count,
-        out_shape=list(out_shape) + sends.out_shape,
-        scratch_shapes=list(scratch) + sends.scratch,
-        input_output_aliases=aliases or {},
-        name=name,
-    )(*operands, *sends.arrays, after)
-    return results[:outs], results[outs:]
-
-
 def first_kernel(x, weights):
     tokens, d = x.shape
     ff = weights["g"].shape[2]
@@ -448,50 +382,17 @@
             dg_ref[:, at] = (dh * (u * (s + sl * (1.0 - s)))).astype(BF16)
             du_ref[:, at] = (dh * sl).astype(BF16)
 
-    return hosted(
+    return pl.pallas_call(
         kernel,
-        tokens // tile,
-        6 * tokens * d * ff,
-        [a, dy, *weights],
-        [rows(tile, d)] * 2 + [ANY] * len(weights),
-        [rows(tile, ff)] * 3,
-        [shaped(tokens, ff)] * 3,
-        scratch_for(*matrices),
-        Sends(),
-        a,
-        "last_layer",
-    )[0]
-
-
-def hidden_back(dy, silu, slope, w, sends, after):
-    tokens, d = dy.shape
-    ff = silu.shape[1]
-    tile, part = min(256, tokens), 256
-    weights = w.operands
-
-    def kernel(dy_ref, s_ref, q_ref, *refs):
-        ins, (dg_ref, du_ref, wd, sems) = refs[: len(weights)], refs[len(weights) :]
-        fetch((w,), ins, (wd,), sems)
-        dyv = dy_ref[...]
-        for j in range(0, ff, part):
-            at = pl.ds(j, part)
-            dh = rounded(dot_nt(dyv, wd[at, :]))
-            dg_ref[:, at] = (dh * q_ref[:, at]).astype(BF16)
-            du_ref[:, at] = (dh * s_ref[:, at]).astype(BF16)
-
-    return hosted(
-        kernel,
-        tokens // tile,
-        2 * tokens * d * ff,
-        [dy, silu, slope, *weights],
-        [rows(tile, d)] + [rows(tile, ff)] * 2 + [ANY] * len(weights),
-        [rows(tile, ff)] * 2,
-        [shaped(tokens, ff)] * 2,
-        scratch_for(w),
-        sends,
-        after,
-        "hidden_back",
-    )
+        grid=(tokens // tile,),
+        cost_estimate=cost(6 * tokens * d * ff),
+        compiler_params=params(),
+        in_specs=[rows(tile, d)] * 2 + [ANY] * len(weights),
+        out_specs=[rows(tile, ff)] * 3,
+        out_shape=[shaped(tokens, ff)] * 3,
+        scratch_shapes=scratch_for(*matrices),
+        name="last_layer",
+    )(a, dy, *weights)
 
 
 def norm_back(da, wide, dres):
@@ -500,147 +401,222 @@
     return (dres + rounded(da * scale - wide * along)).astype(BF16)
 
 
-def input_back(dg, du, h, dres, gate, up, sends, after):
-    tokens, ff = dg.shape
-    d = h.shape[1]
+class Part:
+    def __init__(self, name, term_shape, start, width):
+        self.name, self.start, self.width = name, start, width
+        self.block = term_shape[0] // 4
+
+    def arrays(self):
+        one = shaped(self.block, self.width)
+        return {"r": shaped(2, self.block, self.width), "s": one, "x": one, "b": one, "y": one}
+
+
+def backward(x, dy, a0, a1, h1, hidden0, hidden1, silu, slope, dg1, du1, gate0, up0, down0, gate1, up1):
+    tokens, d = x.shape
+    ff = silu.shape[1]
+    shapes = {"wg": (d, ff), "wu": (d, ff), "wd": (ff, d)}
+    terms = {name + layer: shaped(*shapes[name]) for layer in "10" for name in ("wd", "wg", "wu")}
+    parts = [Part(name, terms[name].shape, 0, terms[name].shape[1]) for name in ("wd1", "wg1", "wu1", "wd0", "wg0")]
+    parts += [Part("wu0", shapes["wu"], n * (ff // 2), ff // 2) for n in range(2)]
+    WD1, WG1, WU1, WD0, WG0, WU0, WU0B = range(7)
+    matrices = {"gate0": gate0, "up0": up0, "down0": down0, "gate1": gate1, "up1": up1}
+    plain = {"x": x, "dy": dy, "a0": a0, "a1": a1, "h1": h1, "hidden0": hidden0, "hidden1": hidden1, "silu": silu, "slope": slope, "dg1": dg1, "du1": du1}
+    operands = list(plain.values()) + operands_of(*matrices.values())
+    made = {"dx": shaped(tokens, d), "dh": shaped(tokens, d), "dg0": shaped(tokens, ff), "du0": shaped(tokens, ff), **terms}
+    part_arrays = [part.arrays() for part in parts]
+    out_shape = list(made.values()) + [one for group in part_arrays for one in group.values()]
     tile = min(256, tokens)
-    weights = operands_of(gate, up)
-
-    def kernel(dg_ref, du_ref, h_ref, r_ref, *refs):
-        ins, (o_ref, wg, wu, sems) = refs[: len(weights)], refs[len(weights) :]
-        fetch((gate, up), ins, (wg, wu), sems)
-        da = rounded(rounded(dot_nt(dg_ref[...], wg[...])) + rounded(dot_nt(du_ref[...], wu[...])))
-        o_ref[...] = norm_back(da, h_ref[...].astype(F32), r_ref[...].astype(F32))
-
-    return hosted(
+    col = min(512, ff)
+
+    def kernel(*refs):
+        refs = list(refs)
+
+        def take(n):
+            taken, refs[:] = refs[:n], refs[n:]
+            return taken
+
+        ref = dict(zip(plain, take(len(plain)), strict=True))
+        weight = {name: take(len(m.operands)) for name, m in matrices.items()}
+        ref.update(zip(made, take(len(made)), strict=True))
+        bufs = [dict(zip(group, take(len(group)), strict=True)) for group in part_arrays]
+        send, recv, load_sems, add_sems = refs
+        at = Place()
+
+        def transfer(n, kind):
+            part, buf = parts[n], bufs[n]
+            base = 4 * n
+            if kind == "mate":
+                cols = pl.ds(part.start, part.width)
+                pairs = [(part_rows(ref[part.name], who * part.block, part.block).at[:, cols], buf["r"].at[k]) for k, who in enumerate((at.mate, at.far_mate))]
+            else:
+                pairs, base = [(buf["s" if kind == "x" else "b"], buf[kind])], base + (2 if kind == "x" else 3)
+            return [
+                pltpu.make_async_remote_copy(src, dst, send.at[base + k], recv.at[base + k], device_id=at.to[kind], device_id_type=MESH)
+                for k, (src, dst) in enumerate(pairs)
+            ]
+
+        def start(n, kind):
+            for copy in transfer(n, kind):
+                copy.start()
+
+        def finish(n, kind):
+            for copy in transfer(n, kind):
+                copy.wait()
+
+        def add(n, which):
+            part, buf = parts[n], bufs[n]
+            k = 1 if which == "s" else 0
+            own = part_rows(ref[part.name], (at.far if k else at.me) * part.block, part.block).at[:, pl.ds(part.start, part.width)]
+            sources = [own, buf["r"].at[k]] + ([] if k else [buf["x"]])
+            size = part.block // 2
+
+            def run(ins, out):
+                loads = []
+                for p in range(2):
+                    loads.append([pltpu.make_async_copy(src.at[pl.ds(p * size, size)], ins.at[q, pl.ds(p * size, size)], add_sems.at[3 * p + q]) for q, src in enumerate(sources)])
+                    for copy in loads[-1]:
+                        copy.start()
+                stores = []
+                for p in range(2):
+                    for copy in loads[p]:
+                        copy.wait()
+                    here = pl.ds(p * size, size)
+                    out[here] = sum(ins[q, here].astype(F32) for q in range(len(sources))).astype(BF16)
+                    stores.append(pltpu.make_async_copy(out.at[here], buf[which].at[here], add_sems.at[6 + p]))
+                    stores[-1].start()
+                for copy in stores:
+                    copy.wait()
+
+            pl.run_scoped(run, pltpu.VMEM((len(sources), part.block, part.width), BF16), pltpu.VMEM((part.block, part.width), BF16))
+
+        def to_x(n):
+            finish(n, "mate")
+            add(n, "s")
+            start(n, "x")
+
+        def to_y(n):
+            finish(n, "x")
+            add(n, "b")
+            start(n, "y")
+
+        def stage(body, steps, in_specs, out_specs, arrays, residents, events=None):
+            def run(*scratch):
+                copies, pairs = [], []
+                for name, space in zip(residents, scratch, strict=True):
+                    if name in matrices:
+                        pairs.append((matrices[name].pairs(weight[name]), space))
+                    else:
+                        copies.append(pltpu.make_async_copy(ref[name], space, load_sems.at[len(copies)]))
+                        copies[-1].start()
+                copies += load(pairs, load_sems, len(copies))
+                for copy in copies:
+                    copy.wait()
+
+                def inner(*blocks):
+                    for when, what in (events or {}).items():
+
+                        @pl.when(pl.program_id(0) == min(when, steps - 1))
+                        def _():
+                            for act, n in what:
+                                act(n)
+
+                    body(scratch, *blocks)
+
+                pltpu.emit_pipeline(inner, grid=(steps,), in_specs=in_specs, out_specs=out_specs)(*(ref[name] for name in arrays))
+
+            shapes_here = [matrices[name].shape if name in matrices else plain[name].shape if name in plain else made[name].shape for name in residents]
+            pl.run_scoped(run, *[pltpu.VMEM(shape, BF16) for shape in shapes_here])
+
+        def grad_in(a, b, out, events=None):
+            def body(scratch, b_ref, o_ref):
+                o_ref[...] = dot_tn(scratch[0][...], b_ref[...]).astype(BF16)
+
+            stage(body, ff // col, [pl.BlockSpec((tokens, col), lambda i: (0, i))], [pl.BlockSpec((d, col), lambda i: (0, i))], (b, out), (a,), events)
+
+        def grad_out(hidden, dres, out, events=None):
+            def body(scratch, h_ref, o_ref):
+                o_ref[...] = dot_tn(h_ref[...], scratch[0][...]).astype(BF16)
+
+            stage(body, ff // col, [pl.BlockSpec((tokens, col), lambda i: (0, i))], [pl.BlockSpec((col, d), lambda i: (i, 0))], (hidden, out), (dres,), events)
+
+        def input_back(dg, du, h, dres, gate, up, out, events=None):
+            def body(scratch, dg_ref, du_ref, h_ref, r_ref, o_ref):
+                da = rounded(rounded(dot_nt(dg_ref[...], scratch[0][...])) + rounded(dot_nt(du_ref[...], scratch[1][...])))
+                o_ref[...] = norm_back(da, h_ref[...].astype(F32), r_ref[...].astype(F32))
+
+            wide, narrow = pl.BlockSpec((tile, ff), lambda i: (i, 0)), pl.BlockSpec((tile, d), lambda i: (i, 0))
+            stage(body, tokens // tile, [wide, wide, narrow, narrow], [narrow], (dg, du, h, dres, out), (gate, up), events)
+
+        def hidden_back(events=None):
+            size = min(256, ff)
+
+            def body(scratch, h_ref, s_ref, q_ref, w_ref, dg_ref, du_ref):
+                dres, wd = scratch
+                w_ref[...] = dot_tn(h_ref[...], dres[...]).astype(BF16)
+                here = pl.ds(pl.multiple_of(pl.program_id(0) * size, size), size)
+                rows_at_once = min(512, tokens)
+
+                @pl.loop(0, tokens // rows_at_once)
+                def _(k):
+                    some = pl.ds(pl.multiple_of(k * rows_at_once, rows_at_once), rows_at_once)
+                    dh = rounded(dot_nt(dres[some], wd[here]))
+                    dg_ref[some] = (dh * q_ref[some]).astype(BF16)
+                    du_ref[some] = (dh * s_ref[some]).astype(BF16)
+
+            tall = pl.BlockSpec((tokens, size), lambda i: (0, i))
+            stage(
+                body,
+                ff // size,
+                [tall] * 3,
+                [pl.BlockSpec((size, d), lambda i: (i, 0)), tall, tall],
+                ("hidden0", "silu", "slope", "wd0", "dg0", "du0"),
+                ("dh", "down0"),
+                events,
+            )
+
+        at.greet(("mate", "x", "y"))
+        grad_out("hidden1", "dy", "wd1")
+        start(WD1, "mate")
+        grad_in("a1", "dg1", "wg1", {2: [(to_x, WD1)]})
+        start(WG1, "mate")
+        grad_in("a1", "du1", "wu1", {2: [(to_x, WG1)], 4: [(to_y, WD1)]})
+        start(WU1, "mate")
+        input_back("dg1", "du1", "h1", "dy", "gate1", "up1", "dh", {3: [(to_x, WU1)], 5: [(to_y, WG1)], 14: [(to_y, WU1)]})
+        hidden_back()
+        start(WD0, "mate")
+        grad_in("a0", "dg0", "wg0", {2: [(to_x, WD0)]})
+        start(WG0, "mate")
+        grad_in("a0", "du0", "wu0", {2: [(to_x, WG0)], 4: [(to_y, WD0)]})
+        start(WU0, "mate")
+        start(WU0B, "mate")
+        input_back(
+            "dg0", "du0", "x", "dh", "gate0", "up0", "dx", {3: [(to_x, WU0), (to_x, WU0B)], 5: [(to_y, WG0)], 10: [(to_y, WU0)], 13: [(to_y, WU0B)]}
+        )
+        for n in range(len(parts)):
+            finish(n, "y")
+
+    results = pl.pallas_call(
         kernel,
-        tokens // tile,
-        4 * tokens * d * ff,
-        [dg, du, h, dres, *weights],
-        [rows(tile, ff)] * 2 + [rows(tile, d)] * 2 + [ANY] * len(weights),
-        [rows(tile, d)],
-        [shaped(tokens, d)],
-        scratch_for(gate, up),
-        sends,
-        after,
-        "input_back",
-    )
-
-
-def input_back_gate(dg, gate, part, parts, sends, after):
-    tokens, ff = dg.shape[0] // parts, dg.shape[1]
-    d = gate.shape[0]
-    tile = min(256, tokens)
-    first = part * (tokens // tile)
-    weights = gate.operands
-
-    def kernel(dg_ref, *refs):
-        ins, (o_ref, wg, sems) = refs[: len(weights)], refs[len(weights) :]
-        fetch((gate,), ins, (wg,), sems)
-        o_ref[...] = dot_nt(dg_ref[...], wg[...]).astype(BF16)
-
-    return hosted(
-        kernel,
-        tokens // tile,
-        2 * tokens * d * ff,
-        [dg, *weights],
-        [pl.BlockSpec((tile, ff), lambda i: (i + first, 0))] + [ANY] * len(weights),
-        [rows(tile, d)],
-        [shaped(tokens, d)],
-        scratch_for(gate),
-        sends,
-        after,
-        f"input_back_gate_{part}",
-    )
-
-
-def input_back_up(du, from_gate, h, dres, up, sends, after):
-    tokens, ff = du.shape
-    d = h.shape[1]
-    tile = min(256, tokens)
-    split = (tokens // tile) // 2
-    weights = up.operands
-
-    def kernel(du_ref, f0_ref, f1_ref, h_ref, r_ref, *refs):
-        ins, (o_ref, wu, sems) = refs[: len(weights)], refs[len(weights) :]
-        fetch((up,), ins, (wu,), sems)
-        first = jnp.where(pl.program_id(0) < split, f0_ref[...].astype(F32), f1_ref[...].astype(F32))
-        da = rounded(first + rounded(dot_nt(du_ref[...], wu[...])))
-        o_ref[...] = norm_back(da, h_ref[...].astype(F32), r_ref[...].astype(F32))
-
-    return hosted(
-        kernel,
-        tokens // tile,
-        2 * tokens * d * ff,
-        [du, *from_gate, h, dres, *weights],
-        [
-            rows(tile, ff),
-            pl.BlockSpec((tile, d), lambda i: (jnp.minimum(i, split - 1), 0)),
-            pl.BlockSpec((tile, d), lambda i: (jnp.maximum(i - split, 0), 0)),
-            rows(tile, d),
-            rows(tile, d),
-        ]
-        + [ANY] * len(weights),
-        [rows(tile, d)],
-        [shaped(tokens, d)],
-        scratch_for(up),
-        sends,
-        after,
-        "input_back_up",
-    )
-
-
-def whole_block(shape):
-    return pl.BlockSpec(shape, lambda i: (0, 0), pipeline_mode=pl.Buffered(1))
-
-
-def grad_in(a, b, sends, after, name, part=0, parts=1):
-    tokens, d = a.shape
-    width = b.shape[1] // parts
-    tile = min(512, width)
-    first = part * (width // tile)
-
-    def kernel(a_ref, b_ref, o_ref):
-        o_ref[...] = dot_tn(a_ref[...], b_ref[...]).astype(BF16)
-
-    (term,), arrived = hosted(
-        kernel,
-        width // tile,
-        2 * tokens * d * width,
-        [a, b],
-        [whole_block((tokens, d)), pl.BlockSpec((tokens, tile), lambda i: (0, i + first))],
-        [pl.BlockSpec((d, tile), lambda i: (0, i))],
-        [shaped(d, width)],
-        [],
-        sends,
-        after,
-        name,
-    )
-    return term, arrived
-
-
-def grad_out(hidden, dy, sends, after, name):
-    tokens, d = dy.shape
-    ff = hidden.shape[1]
-    tile = min(512, ff)
-
-    def kernel(hidden_ref, dy_ref, o_ref):
-        o_ref[...] = dot_tn(hidden_ref[...], dy_ref[...]).astype(BF16)
-
-    (term,), arrived = hosted(
-        kernel,
-        ff // tile,
-        2 * tokens * d * ff,
-        [hidden, dy],
-        [pl.BlockSpec((tokens, tile), lambda i: (0, i)), whole_block((tokens, d))],
-        [rows(tile, d)],
-        [shaped(ff, d)],
-        [],
-        sends,
-        after,
-        name,
-    )
-    return term, arrived
+        cost_estimate=cost(26 * tokens * d * ff),
+        compiler_params=pltpu.CompilerParams(vmem_limit_bytes=62 << 20, collective_id=2, has_side_effects=True),
+        in_specs=[ANY] * len(operands),
+        out_specs=[ANY] * len(out_shape),
+        out_shape=out_shape,
+        scratch_shapes=[
+            pltpu.SemaphoreType.DMA((4 * len(parts),)),
+            pltpu.SemaphoreType.DMA((4 * len(parts),)),
+            pltpu.SemaphoreType.DMA((40,)),
+            pltpu.SemaphoreType.DMA((8,)),
+        ],
+        name="backward",
+    )(*operands)
+    dx = results[0]
+    sums = {}
+    results = results[len(made) :]
+    for n, part in enumerate(parts):
+        group = dict(zip(part_arrays[n], results[5 * n : 5 * n + 5], strict=True))
+        sums.setdefault(part.name, []).append((group["b"], group["y"]))
+    return dx, sums
 
 
 def total(*terms):
@@ -648,16 +624,9 @@
 
 
 def solution(mesh):
-    def block_of(term, which):
-        size = term.shape[0] // 4
-        return lax.dynamic_slice_in_dim(term, which * size, size, 0)
-
     def step(x, dy, w_gate, w_up, w_down):
         x, dy = x[0], dy[0]
         weights = {"g": w_gate, "u": w_up, "d": w_down}
-        me = lax.axis_index("s")
-        far = (me + 2) % 4
-
         (silu, slope, hidden0, a0), gathered = first_kernel(x, weights)
 
         def whole(name, layer):
@@ -670,37 +639,12 @@
             gathered.setdefault((unit.name, unit.layer), []).append((unit, buf))
         gate1, up1, down1 = (whole(name, 1) for name in "gud")
         hidden1, dg1, du1 = last_layer(a1, dy, gate1, up1, down1)
-
-        def for_x(term, received):
-            return total(block_of(term, far), received[1])
-
-        def for_y(term, received, over_x):
-            return total(block_of(term, me), received[0], over_x)
-
-        wd1, _ = grad_out(hidden1, dy, Sends(), dy, "wd1")
-        wg1, (r_wd1,) = grad_in(a1, dg1, Sends((wd1, "term")), dy, "wg1")
-        wu1, (x_wd1, r_wg1) = grad_in(a1, du1, Sends((for_x(wd1, r_wd1), "x"), (wg1, "term")), dy, "wu1")
-        s_wd1 = for_y(wd1, r_wd1, x_wd1)
-        (dh,), (y_wd1, x_wg1, r_wu1) = input_back(dg1, du1, h1, dy, gate1, up1, Sends((s_wd1, "y"), (for_x(wg1, r_wg1), "x"), (wu1, "term")), dy)
-        s_wg1 = for_y(wg1, r_wg1, x_wg1)
-        wd0, (y_wg1, x_wu1) = grad_out(hidden0, dh, Sends((s_wg1, "y"), (for_x(wu1, r_wu1), "x")), dh, "wd0")
-        s_wu1 = for_y(wu1, r_wu1, x_wu1)
-        (dg0, du0), (y_wu1, r_wd0) = hidden_back(dh, silu, slope, down0, Sends((s_wu1, "y"), (wd0, "term")), dh)
-        wg0, (x_wd0,) = grad_in(a0, dg0, Sends((for_x(wd0, r_wd0), "x")), dh, "wg0")
-        s_wd0 = for_y(wd0, r_wd0, x_wd0)
-        wu0, (y_wd0, r_wg0) = grad_in(a0, du0, Sends((s_wd0, "y"), (wg0, "term")), dh, "wu0")
-        (b0,), (x_wg0, r_wu0) = input_back_gate(dg0, gate0, 0, 2, Sends((for_x(wg0, r_wg0), "x"), (wu0, "term")), dh)
-        s_wg0 = for_y(wg0, r_wg0, x_wg0)
-        (b1,), (y_wg0, x_wu0) = input_back_gate(dg0, gate0, 1, 2, Sends((s_wg0, "y"), (for_x(wu0, r_wu0), "x")), b0)
-        s_wu0 = for_y(wu0, r_wu0, x_wu0)
-        (dx,), (y_wu0,) = input_back_up(du0, (b0, b1), x, dh, up0, Sends((s_wu0, "y")), b1)
-
-        return (
-            dx[None],
-            jnp.stack([total(s_wg0, y_wg0), total(s_wg1, y_wg1)]),
-            jnp.stack([total(s_wu0, y_wu0), total(s_wu1, y_wu1)]),
-            jnp.stack([total(s_wd0, y_wd0), total(s_wd1, y_wd1)]),
-        )
+        dx, sums = backward(x, dy, a0, a1, h1, hidden0, hidden1, silu, slope, dg1, du1, gate0, up0, down0, gate1, up1)
+
+        def out(name):
+            return jnp.stack([jnp.concatenate([total(*pair) for pair in sums[name + layer]], 1) for layer in "01"])
+
+        return dx[None], out("wg"), out("wu"), out("wd")
 
     states, cut = P(("rep", "r", "s"), None, None), P(None, "s", None)
     return jax.shard_map(

time: 993 us -> 927 us (0.934)
  other arithmetic: 64.5 us -> 13.3 us
  Pallas kernels: 907 us -> 890 us
    convert_element_type x11 -> x1, other arithmetic: 51.9 us -> 0.54 us  [total(): return sum((t.astype(F32) for t in terms)).astype(BF16)]
    pallas_call x12 -> x2, Pallas kernels: 703 us -> 686 us  [the longest x1 570 us: backward(): pl.pallas_call(kernel, cost_estimate=cost(26 * tokens * d * ff), compiler...]
where the time goes in v2:
time: 927 us; the launch traced here: 918 us
  Pallas kernels  890 us (96%)
  local copies, waits for them, and re-layouts  13.7 us (1%)
  other arithmetic  13.3 us (1%)
    pallas_call x1, Pallas kernels, backward(): pl.pallas_call(kernel, cost_estimate=cost(26 * tokens * d * ff), compiler...  570 us
    pallas_call x1, Pallas kernels, first_kernel(): pl.pallas_call(kernel, grid=(total_steps,), cost_estimate=cost(4 * tokens...  146 us
    pallas_call x1, Pallas kernels, last_layer(): pl.pallas_call(kernel, grid=(tokens // tile,), cost_estimate=cost(6 * tok...  116 us
    pallas_call x1, Pallas kernels, second_kernel(): pl.pallas_call(kernel, grid=(steps,), cost_estimate=cost(2 * tokens * d *...  58 us

profile of v2, /device:TPU:0, one launch (start us, length us, event | category | flops | bytes accessed | tf_op | source)
XLA Modules:
  0.0 918.0 jit_solution(6027406925208227470)
XLA Ops:
  0.6 146.0 %gate_up.1 = (f32[4096,3072]{1,0:T(8,128)}, f32[4096,3072]{1,0:T(8,128)}, bf16[4096,3072]{1,0:T(8,128)(2,1)}, bf16[4096,1280]{1,0:T(8,128)(2,1)}, bf16[1280,768]...) custom-call(bf16[4096,1280]{1,0:T(8,128)(2,1)} %bitcast.16, ...), custom_call_target="tpu_custom_call" | custom-call | flops 64424509440 | bytes 1048576 | tf_op jit(solution)/shard_map/gate_up/pallas_call | solution.py:265
  146.6 58.0 %down.1 = (bf16[4096,1280]{1,0:T(8,128)(2,1)}, bf16[4096,1280]{1,0:T(8,128)(2,1)}, bf16[1280,1536]{1,0:T(8,128)(2,1)}, bf16[3072,640]{1,0:T(8,128)(2,1)}, bf16[3072,640]{1,0:T(8,128)(2,1)}) custom-call(bf16[4096,3072]{1,0:T(8,128)(2,1)} %get-tuple-element.45.hidden_ref.refs_5_, bf16[4096,1280]{1,0:T(8,128)(2,1)} %bitcast.17, bf16[2,768,1280]{2,1,0:T(8,128)(2,1)} %refs_21_.1, ...), custom_call_target="tpu_custom_call" | custom-call | flops 32212254720 | bytes 1048576 | tf_op jit(solution)/shard_map/down/pallas_call | solution.py:338
  204.6 116.1 %last_layer.1 = (bf16[4096,3072]{1,0:T(8,128)(2,1)}, bf16[4096,3072]{1,0:T(8,128)(2,1)}, bf16[4096,3072]{1,0:T(8,128)(2,1)}) custom-call(bf16[4096,1280]{1,0:T(8,128)(2,1)} %get-tuple-element.48.a_ref.refs_3_, bf16[4096,1280]{1,0:T(8,128)(2,1)} %bitcast.19, bf16[2,320,3072]{2,1,0:T(8,128)(2,1)} %refs_24_.1, ...), custom_call_target="tpu_custom_call" | custom-call | flops 96636764160 | bytes 1048576 | tf_op jit(solution)/shard_map/last_layer/pallas_call | solution.py:385
  320.7 569.7 %backward.1 = (bf16[4096,1280]{1,0:T(8,128)(2,1)}, bf16[4096,1280]{1,0:T(8,128)(2,1)}, bf16[4096,3072]{1,0:T(8,128)(2,1)}, bf16[4096,3072]{1,0:T(8,128)(2,1)}, b...) custom-call(bf16[4096,1280]{1,0:T(8,128)(2,1)} %bitcast.18, ...), custom_call_target="tpu_custom_call" | custom-call | flops 418759311360 | bytes 1048576 | tf_op jit(solution)/shard_map/backward/pallas_call | solution.py:598
  890.4 0.0 copy-start.8
  890.5 0.0 copy-start.9
  890.5 0.0 copy-start.10
  890.5 3.0 fusion.2
  893.5 0.2 copy-done.11
  893.7 0.5 add_convert_fusion.5
  894.3 0.2 maximum_bitcast_fusion
  894.5 2.3 pad_maximum_fusion.1
  896.9 0.0 copy-done.4
  896.9 1.2 copy-done.5
  898.0 0.6 copy-done.6
  898.6 0.6 copy-done.7
  899.2 1.6 fusion
  900.9 2.3 pad_maximum_fusion
  903.2 1.2 copy-done.1
  904.4 0.6 copy-done.2
  905.0 0.6 copy-done.3
  905.6 1.0 fusion.3
  906.6 2.3 pad_maximum_fusion.2
  908.9 8.7 copy.10
  (13 shorter events, 0.0 us)
Async XLA Ops:
  890.4 3.0 copy-start.8
  890.5 3.0 copy-start.9
  890.5 3.0 copy-start.10
  890.5 3.2 copy-start.11
  894.5 2.4 copy-start.4
  894.5 3.6 copy-start.5
  894.5 4.1 copy-start.6
  894.5 4.7 copy-start.7
  900.8 2.4 copy-start
  900.8 3.5 copy-start.1
  900.8 4.1 copy-start.2
  900.9 4.7 copy-start.3

commit v3 on v0

v3 whole, which is shorter than its diff:
```python
import jax
import jax.numpy as jnp
from jax import lax
from jax.experimental import pallas as pl
from jax.experimental.pallas import tpu as pltpu
from jax.sharding import PartitionSpec as P

F32, BF16 = jnp.float32, jnp.bfloat16
ANY = pl.BlockSpec(memory_space=pl.ANY)
MESH = pl.DeviceIdType.MESH
NT = (((1,), (1,)), ((), ()))
TN = (((0,), (0,)), ((), ()))


def dot(a, b):
    return jnp.dot(a, b, preferred_element_type=F32)


def dot_nt(a, b):
    return lax.dot_general(a, b, NT, preferred_element_type=F32)


def dot_tn(a, b):
    return lax.dot_general(a, b, TN, preferred_element_type=F32)


def rounded(v):
    return v.astype(BF16).astype(F32)


def sigmoid(g):
    return pl.reciprocal(1.0 + jnp.exp(-g))


def normed(wide):
    return wide * lax.rsqrt(jnp.mean(wide * wide, -1, keepdims=True) + 1e-6)


def shaped(*shape, dtype=BF16):
    return jax.ShapeDtypeStruct(shape, dtype)


class Place:
    def __init__(self):
        self.me, self.y = lax.axis_index("s"), lax.axis_index("r")
        x, c = self.me // 2, self.me % 2
        self.mate, self.far, self.far_mate = 2 * x + 1 - c, 2 * (1 - x) + c, 2 * (1 - x) + 1 - c
        self.to = {"mate": {"s": self.mate}, "x": {"s": self.far}, "y": {"r": 1 - self.y}}

    def greet(self, whom):
        barrier = pltpu.get_barrier_semaphore()
        for name in whom:
            pl.semaphore_signal(barrier, inc=1, device_id=self.to[name], device_id_type=MESH)
        pl.semaphore_wait(barrier, len(whom))


def part_rows(ref, start, size):
    return ref.at[pl.ds(pl.multiple_of(start, 16), size)]


class Unit:
    def __init__(self, name, layer, start, width):
        self.name, self.layer, self.start, self.width = name, layer, start, width


class Mover:
    KINDS = ("own", "x", "y", "straight", "around")

    def __init__(self, units, weights, buffers, send, recv):
        self.units, self.weights, self.buffers, self.send, self.recv = units, weights, buffers, send, recv
        self.at = Place()

    def copy(self, n, kind, arriving=False):
        unit, buf, at = self.units[n], self.buffers[n], self.at
        block = buf.shape[0] // 4
        half = block // 2
        w = self.weights[unit.name].at[unit.layer]
        cols = pl.ds(unit.start, unit.width)
        mine, other = at.y * half, (1 - at.y) * half
        if arriving:
            start, size = {
                "own": (at.mate * block, block),
                "x": (at.far * block + mine, half),
                "y": (at.far * block + other, half),
                "straight": (at.far_mate * block + mine, half),
                "around": (at.far_mate * block + other, half),
            }[kind]
            src = dst = part_rows(buf, start, size)
        elif kind == "own":
            src, dst = w.at[:, cols], part_rows(buf, at.me * block, block)
        elif kind == "x":
            src, dst = w.at[pl.ds(pl.multiple_of(mine, 16), half), cols], part_rows(buf, at.me * block + mine, half)
        else:
            src = dst = part_rows(buf, at.far * block + (other if kind == "around" else mine), half)
        k = self.KINDS.index(kind)
        to = at.to[{"x": "x", "y": "y"}.get(kind, "mate")]
        return pltpu.make_async_remote_copy(src, dst, self.send.at[n, k], self.recv.at[n, k], device_id=to, device_id_type=MESH)

    def start(self, ns, *kinds):
        for n in ns:
            for kind in kinds:
                self.copy(n, kind).start()

    def arrived(self, ns, *kinds):
        for n in ns:
            for kind in kinds:
                self.copy(n, kind, arriving=True).wait_recv()

    def sent(self, ns):
        for n in ns:
            for kind in self.KINDS:
                self.copy(n, kind).wait_send()


def load(pairs, sems, first=0):
    at, made = Place(), []
    for units, scratch in pairs:
        col = 0
        for unit, w, buf in units:
            block = buf.shape[0] // 4
            for n, who in enumerate((at.me, at.mate, at.far, at.far_mate)):
                src = w.at[unit.layer, :, pl.ds(unit.start, unit.width)] if n == 0 else part_rows(buf, who * block, block)
                dst = scratch.at[pl.ds(pl.multiple_of(who * block, 16), block), pl.ds(col, unit.width)]
                made.append(pltpu.make_async_copy(src, dst, sems.at[first + len(made)]))
                made[-1].start()
            col += unit.width
    return made


def norm_back(da, wide, dres):
    scale = lax.rsqrt(jnp.mean(wide * wide, -1, keepdims=True) + 1e-6)
    along = jnp.sum(da * wide, -1, keepdims=True) * (scale * scale * scale) * (1.0 / wide.shape[-1])
    return (dres + rounded(da * scale - wide * along)).astype(BF16)


class Part:
    def __init__(self, name, term_shape, start, width):
        self.name, self.start, self.width = name, start, width
        self.block = term_shape[0] // 4

    def arrays(self):
        one = shaped(self.block, self.width)
        return {"r": shaped(2, self.block, self.width), "s": one, "x": one, "b": one, "y": one}


def everything(x, dy, weights):
    tokens, d = x.shape
    ff = weights["g"].shape[2]
    block = ff // 4
    shapes = {"wg": (d, ff), "wu": (d, ff), "wd": (ff, d)}
    terms = {name + layer: shaped(*shapes[name]) for layer in "10" for name in ("wd", "wg", "wu")}
    parts = [Part(name, terms[name].shape, 0, terms[name].shape[1]) for name in ("wd1", "wg1", "wu1")]
    for name in ("wd0", "wg0", "wu0"):
        width = terms[name].shape[1] // 2
        parts += [Part(name, terms[name].shape, n * width, width) for n in range(2)]
    WD1, WG1, WU1, WD0A, WD0B, WG0A, WG0B, WU0A, WU0B = range(9)
    units, groups = [], []
    for c in range(4):
        groups.append((len(units), len(units) + 1))
        units += [Unit("g", 0, c * block, block), Unit("u", 0, c * block, block)]
    for name, layer in (("d", 0), ("g", 1), ("u", 1), ("d", 1)):
        columns = weights[name].shape[2] // 2
        for n in range(2):
            groups.append((len(units),))
            units.append(Unit(name, layer, n * columns, columns))
    of = {}
    for n, unit in enumerate(units):
        of.setdefault(unit.name + str(unit.layer), []).append(n)
    states, wide = shaped(tokens, d), shaped(tokens, ff)
    made = {name: states for name in ("dx", "dh", "a0", "a1", "h1")} | {name: wide for name in ("hidden0", "hidden1", "dg0", "du0", "dg1", "du1")}
    made |= {name: shaped(tokens, ff, dtype=F32) for name in ("silu", "slope")} | {name: shaped(tokens, block) for name in ("early0", "early1")} | terms
    part_arrays = [part.arrays() for part in parts]
    buffer_shapes = [shaped(4 * weights[unit.name].shape[1], unit.width) for unit in units]
    out_shape = list(made.values()) + buffer_shapes + [one for group in part_arrays for one in group.values()]
    tile = min(256, tokens)
    col = min(512, ff)

    def kernel(*refs):
        refs = list(refs)

        def take(n):
            taken, refs[:] = refs[:n], refs[n:]
            return taken

        ref = dict(zip(("x", "dy"), take(2), strict=True))
        weight = dict(zip(weights, take(len(weights)), strict=True))
        ref.update(zip(made, take(len(made)), strict=True))
        buffers = take(len(units))
        bufs = [dict(zip(group, take(len(group)), strict=True)) for group in part_arrays]
        send, recv, load_sems, add_sems, unit_send, unit_recv = refs
        move = Mover(units, weight, buffers, unit_send, unit_recv)
        at = move.at

        def over_x(k):
            move.arrived(groups[k], "x")
            move.start(groups[k], "y", "straight")
            if k + 2 < len(groups):
                move.start(groups[k + 2], "x")

        def over_y(k):
            move.arrived(groups[k], "y")
            move.start(groups[k], "around")

        def arrived(*ks):
            for k in ks:
                move.arrived(groups[k], "own", "straight", "around")

        def transfer(n, kind):
            part, buf = parts[n], bufs[n]
            base = 4 * n
            if kind == "mate":
                cols = pl.ds(part.start, part.width)
                pairs = [(part_rows(ref[part.name], who * part.block, part.block).at[:, cols], buf["r"].at[k]) for k, who in enumerate((at.mate, at.far_mate))]
            else:
                pairs, base = [(buf["s" if kind == "x" else "b"], buf[kind])], base + (2 if kind == "x" else 3)
            return [
                pltpu.make_async_remote_copy(src, dst, send.at[base + k], recv.at[base + k], device_id=at.to[kind], device_id_type=MESH)
                for k, (src, dst) in enumerate(pairs)
            ]

        def start(n, kind):
            for copy in transfer(n, kind):
                copy.start()

        def finish(n, kind):
            for copy in transfer(n, kind):
                copy.wait()

        def sources(n, which):
            part, buf = parts[n], bufs[n]
            own = part_rows(ref[part.name], (at.far if which == "s" else at.me) * part.block, part.block).at[:, pl.ds(part.start, part.width)]
            return [own, buf["r"].at[1]] if which == "s" else [own, buf["r"].at[0], buf["x"]]

        def sum_loads(n, which, space):
            base = 10 * n + (5 if which == "b" else 0)
            return [pltpu.make_async_copy(src, space.at[q], add_sems.at[base + q]) for q, src in enumerate(sources(n, which))]

        def before_sum(n, which, space):
            finish(n, "mate" if which == "s" else "x")
            for copy in sum_loads(n, which, space):
                copy.start()

        def sum_and_send(n, which, space):
            for copy in sum_loads(n, which, space):
                copy.wait()
            part, stores = parts[n], []
            size = part.block // 2
            for p in range(2):
                here = pl.ds(p * size, size)
                space[0, here] = sum(space[q, here].astype(F32) for q in range(space.shape[0])).astype(BF16)
                stores.append(pltpu.make_async_copy(space.at[0, here], bufs[n][which].at[here], add_sems.at[10 * n + (5 if which == "b" else 0) + 3 + p]))
                stores[-1].start()
            for copy in stores:
                copy.wait()
            start(n, "x" if which == "s" else "y")

        def stage(body, steps, in_specs, out_specs, arrays, residents, events=(), acts=()):
            events = [(min(when, steps - 1), min(when + 1, steps - 1), n, which) for when, n, which in events]

            def run(*scratch):
                scratch, spaces = scratch[: len(residents)], scratch[len(residents) :]
                copies, pairs = [], []
                for what, space in zip(residents, scratch, strict=True):
                    if isinstance(what, str):
                        copies.append(pltpu.make_async_copy(ref[what], space, load_sems.at[len(copies)]))
                        copies[-1].start()
                    else:
                        pairs.append(([(units[n], weight[units[n].name], buffers[n]) for n in what], space))
                copies += load(pairs, load_sems, len(copies))
                for copy in copies:
                    copy.wait()

                def inner(*blocks):
                    now = pl.program_id(0)
                    for (first, then, n, which), space in zip(events, spaces, strict=True):

                        @pl.when(now == first)
                        def _():
                            before_sum(n, which, space)

                        @pl.when(now == then)
                        def _():
                            sum_and_send(n, which, space)

                    for when, act, k in acts:

                        @pl.when(now == min(when, steps - 1))
                        def _():
                            act(k)

                    body(scratch, *blocks)

                pltpu.emit_pipeline(inner, grid=(steps,), in_specs=in_specs, out_specs=out_specs)(*(ref[name] for name in arrays))

            shapes_here = [
                ref[what].shape if isinstance(what, str) else (buffer_shapes[what[0]].shape[0], sum(units[n].width for n in what)) for what in residents
            ]
            shapes_here += [(2 if which == "s" else 3, parts[n].block, parts[n].width) for *_, n, which in events]
            pl.run_scoped(run, *[pltpu.VMEM(shape, BF16) for shape in shapes_here])

        def grad_in(a, b, out, events=()):
            def body(scratch, b_ref, o_ref):
                o_ref[...] = dot_tn(scratch[0][...], b_ref[...]).astype(BF16)

            stage(body, ff // col, [pl.BlockSpec((tokens, col), lambda i: (0, i))], [pl.BlockSpec((d, col), lambda i: (0, i))], (b, out), (a,), events)

        def grad_out(hidden, dres, out, events=()):
            def body(scratch, h_ref, o_ref):
                o_ref[...] = dot_tn(h_ref[...], scratch[0][...]).astype(BF16)

            stage(body, ff // col, [pl.BlockSpec((tokens, col), lambda i: (0, i))], [pl.BlockSpec((col, d), lambda i: (i, 0))], (hidden, out), (dres,), events)

        def input_back(dg, du, h, dres, gate, up, out, events=()):
            def body(scratch, dg_ref, du_ref, h_ref, r_ref, o_ref):
                da = rounded(rounded(dot_nt(dg_ref[...], scratch[0][...])) + rounded(dot_nt(du_ref[...], scratch[1][...])))
                o_ref[...] = norm_back(da, h_ref[...].astype(F32), r_ref[...].astype(F32))

            wide, narrow = pl.BlockSpec((tile, ff), lambda i: (i, 0)), pl.BlockSpec((tile, d), lambda i: (i, 0))
            stage(body, tokens // tile, [wide, wide, narrow, narrow], [narrow], (dg, du, h, dres, out), (of[gate], of[up]), events)

        def hidden_back(events=()):
            size = min(256, ff)

            def body(scratch, h_ref, s_ref, q_ref, w_ref, dg_ref, du_ref):
                dres, wd = scratch
                w_ref[...] = dot_tn(h_ref[...], dres[...]).astype(BF16)
                here = pl.ds(pl.multiple_of(pl.program_id(0) * size, size), size)
                rows_at_once = min(512, tokens)

                @pl.loop(0, tokens // rows_at_once)
                def _(k):
                    some = pl.ds(pl.multiple_of(k * rows_at_once, rows_at_once), rows_at_once)
                    dh = rounded(dot_nt(dres[some], wd[here]))
                    dg_ref[some] = (dh * q_ref[some]).astype(BF16)
                    du_ref[some] = (dh * s_ref[some]).astype(BF16)

            tall = pl.BlockSpec((tokens, size), lambda i: (0, i))
            stage(
                body,
                ff // size,
                [tall] * 3,
                [pl.BlockSpec((size, d), lambda i: (i, 0)), tall, tall],
                ("hidden0", "silu", "slope", "wd0", "dg0", "du0"),
                ("dh", of["d0"]),
                events,
            )

        wide_tile, narrow_tile = pl.BlockSpec((tile, ff), lambda i: (i, 0)), pl.BlockSpec((tile, d), lambda i: (i, 0))
        early_tile = pl.BlockSpec((tile, block), lambda i: (i, 0))
        big = min(512, tokens)

        def early(which, acts):
            def run(space):
                if which:
                    move.arrived(of["d1"], "own")
                    copies, at_col = [], 0
                    for n in of["d1"]:
                        copies.append((part_rows(buffers[n], at.mate * block, block), space.at[:, pl.ds(at_col, units[n].width)]))
                        at_col += units[n].width
                else:
                    copies = [(weight["d"].at[1], space)]
                copies = [pltpu.make_async_copy(src, dst, load_sems.at[n]) for n, (src, dst) in enumerate(copies)]
                for copy in copies:
                    copy.start()
                for copy in copies:
                    copy.wait()

                def body(dy_ref, o_ref, *more):
                    for when, act, k in acts:

                        @pl.when(pl.program_id(0) == min(when, tokens // big - 1))
                        def _():
                            act(k)

                    o_ref[...] = dot_nt(dy_ref[...], space[...]).astype(BF16)

                one, out = pl.BlockSpec((big, d), lambda i: (i, 0)), pl.BlockSpec((big, block), lambda i: (i, 0))
                pltpu.emit_pipeline(body, grid=(tokens // big,), in_specs=[one], out_specs=[out])(ref["dy"], ref[f"early{which}"])

            pl.run_scoped(run, pltpu.VMEM((block, d), BF16))

        def norm_x():
            def body(x_ref, a_ref):
                a_ref[...] = normed(x_ref[...].astype(F32)).astype(BF16)

            one = pl.BlockSpec((big, d), lambda i: (i, 0))
            pltpu.emit_pipeline(body, grid=(tokens // big,), in_specs=[one], out_specs=[one])(ref["x"], ref["a0"])

        def gate_up(first, count, acts):
            width, size = count * block, min(256, block)

            def body(scratch, a_ref, s_ref, q_ref, h_ref):
                wg, wu = scratch
                av = a_ref[...]
                for j in range(0, width, size):
                    here = pl.ds(j, size)
                    g, u = dot(av, wg[:, here]), dot(av, wu[:, here])
                    s = sigmoid(g)
                    sl = g * s
                    s_ref[:, here] = sl
                    q_ref[:, here] = u * (s + sl * (1.0 - s))
                    h_ref[:, here] = (sl * u).astype(BF16)

            out = pl.BlockSpec((big, width), lambda i: (i, first // count))
            weights_here = tuple(of[name][first : first + count] for name in ("g0", "u0"))
            stage(body, tokens // big, [pl.BlockSpec((big, d), lambda i: (i, 0))], [out] * 3, ("a0", "silu", "slope", "hidden0"), weights_here, (), acts)

        def down(acts):
            def body(scratch, hidden_ref, x_ref, h_ref, a_ref):
                out = (x_ref[...].astype(F32) + rounded(dot(hidden_ref[...], scratch[0][...]))).astype(BF16)
                h_ref[...] = out
                a_ref[...] = normed(out.astype(F32)).astype(BF16)

            stage(body, tokens // tile, [wide_tile, narrow_tile], [narrow_tile] * 2, ("hidden0", "x", "h1", "a1"), (of["d0"],), (), acts)

        def last_layer():
            size = min(256, block)

            def body(scratch, a_ref, dy_ref, e0_ref, e1_ref, h_ref, dg_ref, du_ref):
                wg, wu, wd = scratch
                av, dyv = a_ref[...], dy_ref[...]
                for q, who in enumerate((at.me, at.mate, at.far, at.far_mate)):
                    for j in range(0, block, size):
                        here = pl.ds(pl.multiple_of(who * block + j, size), size)
                        g, u = dot(av, wg[:, here]), dot(av, wu[:, here])
                        dh = (e0_ref, e1_ref)[q][:, pl.ds(j, size)].astype(F32) if q < 2 else rounded(dot_nt(dyv, wd[here, :]))
                        s = sigmoid(g)
                        sl = g * s
                        h_ref[:, here] = (sl * u).astype(BF16)
                        dg_ref[:, here] = (dh * (u * (s + sl * (1.0 - s)))).astype(BF16)
                        du_ref[:, here] = (dh * sl).astype(BF16)

            specs = [narrow_tile] * 2 + [early_tile] * 2
            arrays = ("a1", "dy", "early0", "early1", "hidden1", "dg1", "du1")
            stage(body, tokens // tile, specs, [wide_tile] * 3, arrays, (of["g1"], of["u1"], of["d1"]))

        at.greet(("mate", "x", "y"))
        move.start(groups[0] + groups[1], "x")
        move.start(of["d1"], "own")
        for group in groups[:-2]:
            move.start(group, "own")
        early(0, ())
        norm_x()
        early(1, [(1, over_x, 0)])
        over_x(1)
        over_y(0)
        arrived(0)
        gate_up(0, 1, [(3, over_x, 2), (3, over_y, 1), (7, over_x, 3), (7, over_y, 2)])
        arrived(1)
        gate_up(1, 1, [(3, over_x, 4), (3, over_y, 3), (7, over_x, 5), (7, over_y, 4)])
        arrived(2, 3)
        gate_up(2, 2, [(2, over_x, 6), (2, over_y, 5), (4, over_x, 7), (4, over_y, 6), (6, over_x, 8), (6, over_y, 7)])
        arrived(4, 5)
        down([(0, over_x, 9), (0, over_y, 8), (3, over_x, 10), (4, over_y, 9), (7, over_x, 11), (8, over_y, 10), (12, over_y, 11)])
        arrived(6, 7, 8, 9)
        for n in of["d1"]:
            move.arrived((n,), "straight", "around")
        last_layer()

        grad_out("hidden1", "dy", "wd1")
        start(WD1, "mate")
        grad_in("a1", "dg1", "wg1", [(2, WD1, "s")])
        start(WG1, "mate")
        grad_in("a1", "du1", "wu1", [(2, WG1, "s"), (4, WD1, "b")])
        start(WU1, "mate")
        input_back("dg1", "du1", "h1", "dy", "g1", "u1", "dh", [(2, WU1, "s"), (6, WG1, "b"), (14, WU1, "b")])
        hidden_back()
        start(WD0A, "mate")
        start(WD0B, "mate")
        grad_in("a0", "dg0", "wg0", [(1, WD0A, "s"), (1, WD0B, "s")])
        start(WG0A, "mate")
        start(WG0B, "mate")
        grad_in("a0", "du0", "wu0", [(0, WD0A, "b"), (1, WG0A, "s"), (1, WG0B, "s"), (3, WD0B, "b")])
        start(WU0A, "mate")
        start(WU0B, "mate")
        late = [(0, WG0A, "b"), (2, WU0A, "s"), (2, WU0B, "s"), (5, WG0B, "b"), (10, WU0A, "b"), (14, WU0B, "b")]
        input_back("dg0", "du0", "x", "dh", "g0", "u0", "dx", late)
        move.sent(range(len(units)))
        for n in range(len(parts)):
            finish(n, "y")

    results = pl.pallas_call(
        kernel,
        cost_estimate=pl.CostEstimate(flops=34 * tokens * d * ff, bytes_accessed=1 << 30, transcendentals=0),
        compiler_params=pltpu.CompilerParams(vmem_limit_bytes=62 << 20, collective_id=0, has_side_effects=True),
        in_specs=[ANY] * (2 + len(weights)),
        out_specs=[ANY] * len(out_shape),
        out_shape=out_shape,
        scratch_shapes=[
            pltpu.SemaphoreType.DMA((4 * len(parts),)),
            pltpu.SemaphoreType.DMA((4 * len(parts),)),
            pltpu.SemaphoreType.DMA((40,)),
            pltpu.SemaphoreType.DMA((10 * len(parts),)),
            pltpu.SemaphoreType.DMA((len(units), 5)),
            pltpu.SemaphoreType.DMA((len(units), 5)),
        ],
        name="layers",
    )(x, dy, *weights.values())
    dx = results[0]
    sums = {}
    results = results[len(made) + len(units) :]
    for n, part in enumerate(parts):
        group = dict(zip(part_arrays[n], results[5 * n : 5 * n + 5], strict=True))
        sums.setdefault(part.name, []).append((group["b"], group["y"]))
    return dx, sums


def total(*terms):
    return sum(t.astype(F32) for t in terms).astype(BF16)


def solution(mesh):
    def step(x, dy, w_gate, w_up, w_down):
        x, dy = x[0], dy[0]
        weights = {"g": w_gate, "u": w_up, "d": w_down}
        dx, sums = everything(x, dy, weights)

        def out(name):
            return jnp.stack([jnp.concatenate([total(*pair) for pair in sums[name + layer]], 1) for layer in "01"])

        return dx[None], out("wg"), out("wu"), out("wd")

    states, cut = P(("rep", "r", "s"), None, None), P(None, "s", None)
    return jax.shard_map(
        step,
        mesh=mesh,
        in_specs=(states, states) + (cut,) * 3,
        out_specs=(states,) + (P("rep", "s", None),) * 3,
        check_vma=False,
    )
```

time: 1260 us -> 868 us (0.69)
  Pallas kernels: 0 us -> 828 us
  matrix products: 794 us -> 0 us
  waiting for transfers between devices: 338 us -> 0 us
  local copies, waits for them, and re-layouts: 57.8 us -> 15.2 us
  other arithmetic: 45.5 us -> 13.4 us
  between operations: 14.5 us -> 1.33 us
    pallas_call x0 -> x1, Pallas kernels: none -> 828 us  [everything(): pl.pallas_call(kernel, cost_estimate=pl.CostEstimate(flops=34 * tokens *...]
    dot_general x17 -> x0, matrix products: 794 us -> none  [the longest x6 282 us: layer(): up = jnp.dot(a, w['w_up'], preferred_element_type=jnp.float32)]
    psum x1 -> x0, waiting for transfers between devices: 191 us -> none  [summed(): lax.psum(lax.psum_scatter(term, 's', scatter_dimension=0, tiled=True), 'r')]
    reduce_scatter x6 -> x0, waiting for transfers between devices: 87.4 us -> none  [summed(): lax.psum_scatter(term, 's', scatter_dimension=0, tiled=True)]
    all_gather x6 -> x0, waiting for transfers between devices: 58.7 us -> none  [fetched(): lax.all_gather(w[number], 's', axis=0, tiled=True)]
    unnamed x33, local copies, waits for them, and re-layouts: 44.9 us -> 15.2 us
    add_any x1 -> x0, other arithmetic: 14.9 us -> none  [normed(): wide = h.astype(jnp.float32)]
    broadcast_in_dim x1 -> x0, other arithmetic: 14.4 us -> none  [step(): by_h[None]]
  transfers between devices with their start and end apart: 13 -> 0, of which waited for: 8 -> 0; matrix products, arithmetic and copies ran while one was open for 54% -> 0% of each run, Pallas kernels for 0% -> 0%
where the time goes in v3:
time: 868 us; the launch traced here: 858 us
  Pallas kernels  828 us (95%)
  local copies, waits for them, and re-layouts  15.2 us (2%)
  other arithmetic  13.4 us (2%)
    pallas_call x1, Pallas kernels, everything(): pl.pallas_call(kernel, cost_estimate=pl.CostEstimate(flops=34 * tokens *...  828 us

profile of v3, /device:TPU:0, one launch (start us, length us, event | category | flops | bytes accessed | tf_op | source)
XLA Modules:
  0.0 858.1 jit_solution(5845280018331325598)
XLA Ops:
  0.6 828.1 %layers.1 = (bf16[4096,1280]{1,0:T(8,128)(2,1)}, bf16[4096,1280]{1,0:T(8,128)(2,1)}, bf16[4096,1280]{1,0:T(8,128)(2,1)}, bf16[4096,1280]{1,0:T(8,128)(2,1)}, bf1...) custom-call(bf16[4096,1280]{1,0:T(8,128)(2,1)} %bitcast.16, ...), custom_call_target="tpu_custom_call" | custom-call | flops 547608330240 | bytes 1073741824 | tf_op jit(solution)/shard_map/layers/pallas_call | solution.py:482
  828.8 2.8 fusion.2
  831.7 0.3 copy-done.15
  832.0 0.5 add_convert_fusion.7
  832.6 0.2 maximum_bitcast_fusion
  832.8 0.9 copy-done.8
  833.8 0.3 copy-done.9
  834.1 0.3 copy-done.10
  834.4 0.3 copy-done.11
  834.7 0.5 add_convert_fusion.5
  835.2 0.2 maximum_bitcast_fusion.1
  835.5 0.9 copy-done.4
  836.4 0.3 copy-done.5
  836.7 0.3 copy-done.6
  837.0 0.3 copy-done.7
  837.3 0.5 add_convert_fusion.3
  838.0 2.3 pad_maximum_fusion.2
  840.4 1.2 copy-done.1
  841.5 0.6 copy-done.2
  842.1 0.6 copy-done.3
  842.7 1.6 fusion
  844.3 2.3 pad_maximum_fusion
  846.6 2.3 pad_maximum_fusion.1
  848.8 8.7 %copy.10 = bf16[1,4096,1280]{2,1,0:T(8,128)(2,1)} copy(bf16[1,4096,1280]{2,1,0:T(8,128)(2,1)} %bitcast.15) | data formatting | bytes 20971520
  (21 shorter events, 0.3 us)
Async XLA Ops:
  828.8 2.8 copy-start.12
  828.8 2.8 copy-start.13
  828.8 3.0 copy-start.14
  828.8 3.2 copy-start.15
  832.6 1.2 copy-start.8
  832.6 1.5 copy-start.9
  832.6 1.8 copy-start.10
  832.6 2.1 copy-start.11
  835.2 1.2 copy-start.4
  835.2 1.5 copy-start.5
  835.2 1.8 copy-start.6
  835.2 2.1 copy-start.7
  838.0 2.4 copy-start
  838.0 3.5 copy-start.1
  838.0 4.1 copy-start.2
  838.0 4.7 copy-start.3

commit v4 on v3

--- a/solution.py
+++ b/solution.py
@@ -254,24 +254,48 @@
                 copy.wait()
             start(n, "x" if which == "s" else "y")
 
-        def stage(body, steps, in_specs, out_specs, arrays, residents, events=(), acts=()):
+        def fetches(residents, scratch, base=0):
+            copies, pairs = [], []
+            for what, space in zip(residents, scratch, strict=True):
+                if isinstance(what, str):
+                    copies.append(pltpu.make_async_copy(ref[what], space, load_sems.at[base + len(copies)]))
+                    copies[-1].start()
+                else:
+                    pairs.append(([(units[n], weight[units[n].name], buffers[n]) for n in what], space))
+            return copies + load(pairs, load_sems, base + len(copies))
+
+        def spaces_for(residents):
+            return [
+                pltpu.VMEM(ref[what].shape if isinstance(what, str) else (buffer_shapes[what[0]].shape[0], sum(units[n].width for n in what)), BF16)
+                for what in residents
+            ]
+
+        def ahead(residents, before, after, base=40):
+            def run(*scratch):
+                copies = fetches(residents, scratch, base)
+                before()
+                for copy in copies:
+                    copy.wait()
+                after(scratch)
+
+            pl.run_scoped(run, *spaces_for(residents))
+
+        def stage(body, steps, in_specs, out_specs, arrays, residents, events=(), acts=(), ready=None):
             events = [(min(when, steps - 1), min(when + 1, steps - 1), n, which) for when, n, which in events]
 
             def run(*scratch):
                 scratch, spaces = scratch[: len(residents)], scratch[len(residents) :]
-                copies, pairs = [], []
-                for what, space in zip(residents, scratch, strict=True):
-                    if isinstance(what, str):
-                        copies.append(pltpu.make_async_copy(ref[what], space, load_sems.at[len(copies)]))
-                        copies[-1].start()
-                    else:
-                        pairs.append(([(units[n], weight[units[n].name], buffers[n]) for n in what], space))
-                copies += load(pairs, load_sems, len(copies))
-                for copy in copies:
-                    copy.wait()
+                copies = fetches(residents, scratch)
 
                 def inner(*blocks):
                     now = pl.program_id(0)
+                    if copies:
+
+                        @pl.when(now == 0)
+                        def _():
+                            for copy in copies:
+                                copy.wait()
+
                     for (first, then, n, which), space in zip(events, spaces, strict=True):
 
                         @pl.when(now == first)
@@ -288,35 +312,35 @@
                         def _():
                             act(k)
 
-                    body(scratch, *blocks)
+                    body(ready or scratch, *blocks)
 
                 pltpu.emit_pipeline(inner, grid=(steps,), in_specs=in_specs, out_specs=out_specs)(*(ref[name] for name in arrays))
 
-            shapes_here = [
-                ref[what].shape if isinstance(what, str) else (buffer_shapes[what[0]].shape[0], sum(units[n].width for n in what)) for what in residents
-            ]
-            shapes_here += [(2 if which == "s" else 3, parts[n].block, parts[n].width) for *_, n, which in events]
-            pl.run_scoped(run, *[pltpu.VMEM(shape, BF16) for shape in shapes_here])
+            sums = [pltpu.VMEM((2 if which == "s" else 3, parts[n].block, parts[n].width), BF16) for *_, n, which in events]
+            if residents or sums:
+                pl.run_scoped(run, *spaces_for(residents), *sums)
+            else:
+                run()
 
         def grad_in(a, b, out, events=()):
-            def body(scratch, b_ref, o_ref):
-                o_ref[...] = dot_tn(scratch[0][...], b_ref[...]).astype(BF16)
-
-            stage(body, ff // col, [pl.BlockSpec((tokens, col), lambda i: (0, i))], [pl.BlockSpec((d, col), lambda i: (0, i))], (b, out), (a,), events)
-
-        def grad_out(hidden, dres, out, events=()):
+            def body(spaces, b_ref, o_ref):
+                o_ref[...] = dot_tn(a[...], b_ref[...]).astype(BF16)
+
+            stage(body, ff // col, [pl.BlockSpec((tokens, col), lambda i: (0, i))], [pl.BlockSpec((d, col), lambda i: (0, i))], (b, out), (), events)
+
+        def grad_out(ready, hidden, out):
             def body(scratch, h_ref, o_ref):
                 o_ref[...] = dot_tn(h_ref[...], scratch[0][...]).astype(BF16)
 
-            stage(body, ff // col, [pl.BlockSpec((tokens, col), lambda i: (0, i))], [pl.BlockSpec((col, d), lambda i: (i, 0))], (hidden, out), (dres,), events)
-
-        def input_back(dg, du, h, dres, gate, up, out, events=()):
+            stage(body, ff // col, [pl.BlockSpec((tokens, col), lambda i: (0, i))], [pl.BlockSpec((col, d), lambda i: (i, 0))], (hidden, out), (), ready=ready)
+
+        def input_back(ready, dg, du, h, dres, out, events=()):
             def body(scratch, dg_ref, du_ref, h_ref, r_ref, o_ref):
                 da = rounded(rounded(dot_nt(dg_ref[...], scratch[0][...])) + rounded(dot_nt(du_ref[...], scratch[1][...])))
                 o_ref[...] = norm_back(da, h_ref[...].astype(F32), r_ref[...].astype(F32))
 
             wide, narrow = pl.BlockSpec((tile, ff), lambda i: (i, 0)), pl.BlockSpec((tile, d), lambda i: (i, 0))
-            stage(body, tokens // tile, [wide, wide, narrow, narrow], [narrow], (dg, du, h, dres, out), (of[gate], of[up]), events)
+            stage(body, tokens // tile, [wide, wide, narrow, narrow], [narrow], (dg, du, h, dres, out), (), events, ready=ready)
 
         def hidden_back(events=()):
             size = min(256, ff)
@@ -365,26 +389,28 @@
                 for copy in copies:
                     copy.wait()
 
-                def body(dy_ref, o_ref, *more):
+                def body(*blocks):
                     for when, act, k in acts:
 
                         @pl.when(pl.program_id(0) == min(when, tokens // big - 1))
                         def _():
                             act(k)
 
+                    if which:
+                        dy_ref, o_ref = blocks
+                    else:
+                        dy_ref, x_ref, o_ref, a_ref = blocks
+                        a_ref[...] = normed(x_ref[...].astype(F32)).astype(BF16)
                     o_ref[...] = dot_nt(dy_ref[...], space[...]).astype(BF16)
 
                 one, out = pl.BlockSpec((big, d), lambda i: (i, 0)), pl.BlockSpec((big, block), lambda i: (i, 0))
-                pltpu.emit_pipeline(body, grid=(tokens // big,), in_specs=[one], out_specs=[out])(ref["dy"], ref[f"early{which}"])
+                if which:
+                    pltpu.emit_pipeline(body, grid=(tokens // big,), in_specs=[one], out_specs=[out])(ref["dy"], ref["early1"])
+                else:
+                    run_both = pltpu.emit_pipeline(body, grid=(tokens // big,), in_specs=[one, one], out_specs=[out, one])
+                    run_both(ref["dy"], ref["x"], ref["early0"], ref["a0"])
 
             pl.run_scoped(run, pltpu.VMEM((block, d), BF16))
-
-        def norm_x():
-            def body(x_ref, a_ref):
-                a_ref[...] = normed(x_ref[...].astype(F32)).astype(BF16)
-
-            one = pl.BlockSpec((big, d), lambda i: (i, 0))
-            pltpu.emit_pipeline(body, grid=(tokens // big,), in_specs=[one], out_specs=[one])(ref["x"], ref["a0"])
 
         def gate_up(first, count, acts):
             width, size = count * block, min(256, block)
@@ -440,8 +466,7 @@
         for group in groups[:-2]:
             move.start(group, "own")
         early(0, ())
-        norm_x()
-        early(1, [(1, over_x, 0)])
+        early(1, [(2, over_x, 0)])
         over_x(1)
         over_y(0)
         arrived(0)
@@ -455,26 +480,47 @@
         arrived(6, 7, 8, 9)
         for n in of["d1"]:
             move.arrived((n,), "straight", "around")
-        last_layer()
-
-        grad_out("hidden1", "dy", "wd1")
-        start(WD1, "mate")
-        grad_in("a1", "dg1", "wg1", [(2, WD1, "s")])
-        start(WG1, "mate")
-        grad_in("a1", "du1", "wu1", [(2, WG1, "s"), (4, WD1, "b")])
-        start(WU1, "mate")
-        input_back("dg1", "du1", "h1", "dy", "g1", "u1", "dh", [(2, WU1, "s"), (6, WG1, "b"), (14, WU1, "b")])
+        def first_grads(spaces):
+            ahead(("a1",), lambda: grad_out(spaces, "hidden1", "wd1"), other_grads_1, 80)
+
+        def other_grads_1(spaces):
+            start(WD1, "mate")
+            grad_in(spaces[0], "dg1", "wg1", [(2, WD1, "s")])
+            start(WG1, "mate")
+            grad_in(spaces[0], "du1", "wu1", [(2, WG1, "s"), (4, WD1, "b")])
+            start(WU1, "mate")
+
+        def settled(names, spaces):
+            for copy in fetches([of[name] for name in names], spaces):
+                copy.wait()
+            return spaces
+
+        def other_grads_0():
+            def run(space):
+                copies = fetches(("a0",), (space,))
+                for copy in copies:
+                    copy.wait()
+                grad_in(space, "dg0", "wg0", [(1, WD0A, "s"), (1, WD0B, "s")])
+                start(WG0A, "mate")
+                start(WG0B, "mate")
+                grad_in(space, "du0", "wu0", [(0, WD0A, "b"), (1, WG0A, "s"), (1, WG0B, "s"), (3, WD0B, "b")])
+                start(WU0A, "mate")
+                start(WU0B, "mate")
+
+            pl.run_scoped(run, *spaces_for(("a0",)))
+
+        ahead(("dy",), last_layer, first_grads)
+        pl.run_scoped(
+            lambda *spaces: input_back(
+                settled(("g1", "u1"), spaces), "dg1", "du1", "h1", "dy", "dh", [(2, WU1, "s"), (6, WG1, "b"), (14, WU1, "b")]
+            ),
+            *spaces_for((of["g1"], of["u1"])),
+        )
         hidden_back()
         start(WD0A, "mate")
         start(WD0B, "mate")
-        grad_in("a0", "dg0", "wg0", [(1, WD0A, "s"), (1, WD0B, "s")])
-        start(WG0A, "mate")
-        start(WG0B, "mate")
-        grad_in("a0", "du0", "wu0", [(0, WD0A, "b"), (1, WG0A, "s"), (1, WG0B, "s"), (3, WD0B, "b")])
-        start(WU0A, "mate")
-        start(WU0B, "mate")
         late = [(0, WG0A, "b"), (2, WU0A, "s"), (2, WU0B, "s"), (5, WG0B, "b"), (10, WU0A, "b"), (14, WU0B, "b")]
-        input_back("dg0", "du0", "x", "dh", "g0", "u0", "dx", late)
+        ahead((of["g0"], of["u0"]), other_grads_0, lambda spaces: input_back(spaces, "dg0", "du0", "x", "dh", "dx", late))
         move.sent(range(len(units)))
         for n in range(len(parts)):
             finish(n, "y")
@@ -489,7 +535,7 @@
         scratch_shapes=[
             pltpu.SemaphoreType.DMA((4 * len(parts),)),
             pltpu.SemaphoreType.DMA((4 * len(parts),)),
-            pltpu.SemaphoreType.DMA((40,)),
+            pltpu.SemaphoreType.DMA((81,)),
             pltpu.SemaphoreType.DMA((10 * len(parts),)),
             pltpu.SemaphoreType.DMA((len(units), 5)),
             pltpu.SemaphoreType.DMA((len(units), 5)),

time: 868 us -> 847 us (0.976)
  Pallas kernels: 828 us -> 808 us
    pallas_call x1, Pallas kernels: 828 us -> 808 us  [everything(): pl.pallas_call(kernel, cost_estimate=pl.CostEstimate(flops=34 * tokens *...]
where the time goes in v4:
time: 847 us; the launch traced here: 838 us
  Pallas kernels  808 us (95%)
  local copies, waits for them, and re-layouts  15.2 us (2%)
  other arithmetic  13.4 us (2%)
    pallas_call x1, Pallas kernels, everything(): pl.pallas_call(kernel, cost_estimate=pl.CostEstimate(flops=34 * tokens *...  808 us

profile of v4, /device:TPU:0, one launch (start us, length us, event | category | flops | bytes accessed | tf_op | source)
XLA Modules:
  0.0 837.8 jit_solution(1648734549766497679)
XLA Ops:
  0.6 807.8 %layers.1 = (bf16[4096,1280]{1,0:T(8,128)(2,1)}, bf16[4096,1280]{1,0:T(8,128)(2,1)}, bf16[4096,1280]{1,0:T(8,128)(2,1)}, bf16[4096,1280]{1,0:T(8,128)(2,1)}, bf1...) custom-call(bf16[4096,1280]{1,0:T(8,128)(2,1)} %bitcast.16, ...), custom_call_target="tpu_custom_call" | custom-call | flops 547608330240 | bytes 1073741824 | tf_op jit(solution)/shard_map/layers/pallas_call | solution.py:528
  808.5 2.8 fusion.2
  811.4 0.3 copy-done.15
  811.7 0.5 add_convert_fusion.7
  812.3 0.2 maximum_bitcast_fusion
  812.5 0.9 copy-done.8
  813.5 0.3 copy-done.9
  813.8 0.3 copy-done.10
  814.1 0.3 copy-done.11
  814.4 0.5 add_convert_fusion.5
  815.0 0.2 maximum_bitcast_fusion.1
  815.2 0.9 copy-done.4
  816.1 0.3 copy-done.5
  816.4 0.3 copy-done.6
  816.7 0.3 copy-done.7
  817.0 0.5 add_convert_fusion.3
  817.7 2.3 pad_maximum_fusion.2
  820.1 1.2 copy-done.1
  821.2 0.6 copy-done.2
  821.8 0.6 copy-done.3
  822.4 1.6 fusion
  824.0 2.3 pad_maximum_fusion
  826.3 2.3 pad_maximum_fusion.1
  828.5 8.7 %copy.10 = bf16[1,4096,1280]{2,1,0:T(8,128)(2,1)} copy(bf16[1,4096,1280]{2,1,0:T(8,128)(2,1)} %bitcast.15) | data formatting | bytes 20971520
  (21 shorter events, 0.3 us)
Async XLA Ops:
  808.5 2.8 copy-start.12
  808.5 2.8 copy-start.13
  808.5 3.0 copy-start.14
  808.5 3.2 copy-start.15
  812.3 1.2 copy-start.8
  812.3 1.5 copy-start.9
  812.3 1.8 copy-start.10
  812.3 2.1 copy-start.11
  814.9 1.2 copy-start.4
  814.9 1.5 copy-start.5
  814.9 1.8 copy-start.6
  814.9 2.1 copy-start.7
  817.7 2.4 copy-start
  817.7 3.5 copy-start.1
  817.7 4.1 copy-start.2
  817.7 4.7 copy-start.3
